TPU v7x, 32 devices: a whole 2x2x4 slice. The times are simulated.
32 devices in a mesh: fsdp: 8 (over z, y), seq: 4 (over x, core).
Axes of the slice: x: 2, y: 2, z: 4, core: 2. Of those that a mesh axis runs over, the one named last changes fastest.
Arguments:
- tokens: bfloat16 [8, 1024, 1152], P('fsdp', 'seq'), may hold values from -6 to 6
- condition: float32 [8, 1152], P('fsdp'), may hold values from -6 to 6
- w_ada: bfloat16 [1152, 6912], P('fsdp'), may hold values from -0.1875 to 0.1875
- b_ada: bfloat16 [6912], P('fsdp'), may hold values from -3 to 3
- w_qkv: bfloat16 [1152, 3456], P('fsdp'), may hold values from -0.1875 to 0.1875
- b_qv: bfloat16 [2, 1152], P(None, 'fsdp'), may hold values from -3 to 3
- w_out: bfloat16 [1152, 1152], P('fsdp'), may hold values from -0.75 to 0.75
- b_out: bfloat16 [1152], P('fsdp'), may hold values from -3 to 3
- w_up: bfloat16 [1152, 4608], P('fsdp'), may hold values from -0.1875 to 0.1875
- b_up: bfloat16 [4608], P('fsdp'), may hold values from -3 to 3
- w_down: bfloat16 [4608, 1152], P('fsdp'), may hold values from -0.09375 to 0.09375
- b_down: bfloat16 [1152], P('fsdp'), may hold values from -3 to 3
- grad_output: bfloat16 [8, 1024, 1152], P('fsdp', 'seq'), may hold values from -6 to 6
Outputs:
- output: bfloat16 [8, 1024, 1152], P('fsdp', 'seq')
- grad_tokens: bfloat16 [8, 1024, 1152], P('fsdp', 'seq')
- grad_condition: float32 [8, 1152], P('fsdp')
- grad_w_ada: float32 [1152, 6912], P('fsdp')
- grad_b_ada: float32 [6912], P('fsdp')
- grad_w_qkv: float32 [1152, 3456], P('fsdp')
- grad_b_qv: float32 [2, 1152], P(None, 'fsdp')
- grad_w_out: float32 [1152, 1152], P('fsdp')
- grad_b_out: float32 [1152], P('fsdp')
- grad_w_up: float32 [1152, 4608], P('fsdp')
- grad_b_up: float32 [4608], P('fsdp')
- grad_w_down: float32 [4608, 1152], P('fsdp')
- grad_b_down: float32 [1152], P('fsdp')
All inputs are finite; a program needn't handle non-finite values.
Results may differ from a plain program's by a relative error of at most 0.018.
Values may be sent and summed in bfloat16 or wider, within the bound.
A program may use at most 320 MiB of HBM per device.

v0:
```python
import jax
import jax.numpy as jnp
from jax import lax
from jax.sharding import PartitionSpec as P

HD = 72


EPSILON = 1e-06
GELU_C = 0.7978845608028654


def layer_norm(values):
    mean_val = jnp.mean(values, axis=-1, keepdims=True)
    centred = values - mean_val
    inv_std = lax.rsqrt(jnp.mean(centred * centred, axis=-1, keepdims=True) + EPSILON)
    return (centred * inv_std, inv_std)


def norm_back(grad_norm, normed, inv_std):
    first = jnp.mean(grad_norm, axis=-1, keepdims=True)
    second = jnp.mean(grad_norm * normed, axis=-1, keepdims=True)
    return inv_std * (grad_norm - first - normed * second)


def gelu_tanh(values):
    inner = GELU_C * (values + 0.044715 * values * values * values)
    return 0.5 * values * (1.0 + jnp.tanh(inner))


def gelu_slope(values):
    inner = GELU_C * (values + 0.044715 * values * values * values)
    tanh_val = jnp.tanh(inner)
    return 0.5 * (1.0 + tanh_val) + 0.5 * values * (1.0 - tanh_val * tanh_val) * GELU_C * (
        1.0 + 3.0 * 0.044715 * values * values
    )


def matmul(left, right):
    return jnp.dot(left, right, preferred_element_type=jnp.float32)


def matmul_tn(left, right):
    return lax.dot_general(
        left, right, (((0,), (0,)), ((), ())), preferred_element_type=jnp.float32
    )


def matmul_nt(left, right):
    return lax.dot_general(
        left, right, (((1,), (1,)), ((), ())), preferred_element_type=jnp.float32
    )


def head_scores(query, key):
    factor = HD ** (-0.5)
    return jnp.einsum("qhd,khd->hqk", query, key, preferred_element_type=jnp.float32) * factor


def attend_latent(items):
    query, key, value = items
    seq_full = query.shape[0]
    heads_here = query.shape[1] // HD
    query = query.reshape(seq_full, heads_here, HD)
    key = key.reshape(seq_full, heads_here, HD)
    value = value.reshape(seq_full, heads_here, HD)
    scores = head_scores(query, key)
    highest = jnp.max(scores, axis=-1, keepdims=True)
    log_total = highest + jnp.log(jnp.sum(jnp.exp(scores - highest), axis=-1, keepdims=True))
    probs = jnp.exp(scores - log_total).astype(jnp.bfloat16)
    mixed = jnp.einsum("hqk,khd->qhd", probs, value, preferred_element_type=jnp.float32)
    return (mixed.astype(jnp.bfloat16).reshape(seq_full, heads_here * HD), log_total)


def attend_latent_back(items):
    query, key, value, mixed, log_total, grad_mix = items
    factor = HD ** (-0.5)
    seq_full = query.shape[0]
    heads_here = query.shape[1] // HD
    shape_heads = (seq_full, heads_here, HD)
    query = query.reshape(shape_heads)
    key = key.reshape(shape_heads)
    value = value.reshape(shape_heads)
    mixed = mixed.reshape(shape_heads)
    grad_mix = grad_mix.reshape(shape_heads)
    probs = jnp.exp(head_scores(query, key) - log_total)
    delta = jnp.sum(grad_mix.astype(jnp.float32) * mixed.astype(jnp.float32), axis=-1)
    grad_probs = jnp.einsum("qhd,khd->hqk", grad_mix, value, preferred_element_type=jnp.float32)
    grad_scores = (probs * (grad_probs - jnp.transpose(delta)[:, :, None]) * factor).astype(
        jnp.bfloat16
    )
    grad_query = jnp.einsum("hqk,khd->qhd", grad_scores, key, preferred_element_type=jnp.float32)
    grad_key = jnp.einsum("hqk,qhd->khd", grad_scores, query, preferred_element_type=jnp.float32)
    grad_value = jnp.einsum(
        "hqk,qhd->khd", probs.astype(jnp.bfloat16), grad_mix, preferred_element_type=jnp.float32
    )
    flat = (seq_full, heads_here * HD)
    return (
        grad_query.astype(jnp.bfloat16).reshape(flat),
        grad_key.astype(jnp.bfloat16).reshape(flat),
        grad_value.astype(jnp.bfloat16).reshape(flat),
    )


def token_sums(values):
    return jnp.sum(values, axis=1)


def local(
    tokens,
    condition,
    w_ada,
    b_ada,
    w_qkv,
    b_qv,
    w_out,
    b_out,
    w_up,
    b_up,
    w_down,
    b_down,
    grad_output,
):
    lat_dev, seq_loc, width = tokens.shape
    row_count = lat_dev * seq_loc
    full_qkv, full_bqv, full_out, full_bout, full_up, full_bup, full_down, full_bdown, full_bada = (
        lax.all_gather(w_qkv, "fsdp", axis=0, tiled=True),
        lax.all_gather(b_qv, "fsdp", axis=1, tiled=True),
        lax.all_gather(w_out, "fsdp", axis=0, tiled=True),
        lax.all_gather(b_out, "fsdp", axis=0, tiled=True),
        lax.all_gather(w_up, "fsdp", axis=0, tiled=True),
        lax.all_gather(b_up, "fsdp", axis=0, tiled=True),
        lax.all_gather(w_down, "fsdp", axis=0, tiled=True),
        lax.all_gather(b_down, "fsdp", axis=0, tiled=True),
        lax.all_gather(b_ada, "fsdp", axis=0, tiled=True),
    )
    attn_width = full_out.shape[0]
    cond_sig = jax.nn.sigmoid(condition)
    cond_act = (condition * cond_sig).astype(jnp.bfloat16)
    full_ada = lax.all_gather(w_ada, "fsdp", axis=0, tiled=True)
    mods = matmul(cond_act, full_ada) + full_bada.astype(jnp.float32)
    mods = mods.reshape(lat_dev, 6, 1, width)
    shift_attn, scale_attn, gate_attn = (mods[:, 0], mods[:, 1], mods[:, 2])
    shift_ff, scale_ff, gate_ff = (mods[:, 3], mods[:, 4], mods[:, 5])
    source = tokens.astype(jnp.float32)
    normed1, inv1 = layer_norm(source)
    hidden1 = (
        (normed1 * (1.0 + scale_attn) + shift_attn).astype(jnp.bfloat16).reshape(row_count, width)
    )
    qkv = matmul(hidden1, full_qkv)
    tok_shape = (lat_dev, seq_loc, attn_width)
    query = (
        (qkv[:, :attn_width] + full_bqv[0].astype(jnp.float32))
        .astype(jnp.bfloat16)
        .reshape(tok_shape)
    )
    key = qkv[:, attn_width : 2 * attn_width].astype(jnp.bfloat16).reshape(tok_shape)
    value = (
        (qkv[:, 2 * attn_width :] + full_bqv[1].astype(jnp.float32))
        .astype(jnp.bfloat16)
        .reshape(tok_shape)
    )
    heads_q, heads_k, heads_v = (
        lax.all_to_all(query, "seq", split_axis=2, concat_axis=1, tiled=True),
        lax.all_to_all(key, "seq", split_axis=2, concat_axis=1, tiled=True),
        lax.all_to_all(value, "seq", split_axis=2, concat_axis=1, tiled=True),
    )
    mixed_heads, log_totals = lax.map(attend_latent, (heads_q, heads_k, heads_v))
    attn_mix = lax.all_to_all(mixed_heads, "seq", split_axis=1, concat_axis=2, tiled=True).reshape(
        row_count, attn_width
    )
    attn_out = (matmul(attn_mix, full_out) + full_bout.astype(jnp.float32)).reshape(
        lat_dev, seq_loc, width
    )
    resid1 = source + gate_attn * attn_out
    normed2, inv2 = layer_norm(resid1)
    hidden2 = (normed2 * (1.0 + scale_ff) + shift_ff).astype(jnp.bfloat16).reshape(row_count, width)
    pre_act = matmul(hidden2, full_up) + full_bup.astype(jnp.float32)
    activated = gelu_tanh(pre_act).astype(jnp.bfloat16)
    ff_out = (matmul(activated, full_down) + full_bdown.astype(jnp.float32)).reshape(
        lat_dev, seq_loc, width
    )
    output = (resid1 + gate_ff * ff_out).astype(jnp.bfloat16)
    back_qkv, back_out, back_up, back_down = (
        lax.all_gather(w_qkv, "fsdp", axis=0, tiled=True),
        lax.all_gather(w_out, "fsdp", axis=0, tiled=True),
        lax.all_gather(w_up, "fsdp", axis=0, tiled=True),
        lax.all_gather(w_down, "fsdp", axis=0, tiled=True),
    )
    grad_y = grad_output.astype(jnp.float32)
    grad_ff = (grad_y * gate_ff).reshape(row_count, width)
    grad_ff_low = grad_ff.astype(jnp.bfloat16)
    grad_w_down = matmul_tn(activated, grad_ff_low)
    grad_b_down = jnp.sum(grad_ff, axis=0)
    grad_pre = matmul_nt(grad_ff_low, back_down) * gelu_slope(pre_act)
    grad_pre_low = grad_pre.astype(jnp.bfloat16)
    grad_w_up = matmul_tn(hidden2, grad_pre_low)
    grad_b_up = jnp.sum(grad_pre, axis=0)
    grad_h2 = matmul_nt(grad_pre_low, back_up).reshape(lat_dev, seq_loc, width)
    grad_resid1 = grad_y + norm_back(grad_h2 * (1.0 + scale_ff), normed2, inv2)
    grad_attn = (grad_resid1 * gate_attn).reshape(row_count, width)
    grad_attn_low = grad_attn.astype(jnp.bfloat16)
    grad_w_out = matmul_tn(attn_mix, grad_attn_low)
    grad_b_out = jnp.sum(grad_attn, axis=0)
    grad_mix = matmul_nt(grad_attn_low, back_out).astype(jnp.bfloat16).reshape(tok_shape)
    grad_mix_heads = lax.all_to_all(grad_mix, "seq", split_axis=2, concat_axis=1, tiled=True)
    grad_qh, grad_kh, grad_vh = lax.map(
        attend_latent_back, (heads_q, heads_k, heads_v, mixed_heads, log_totals, grad_mix_heads)
    )
    grad_q, grad_k, grad_v = (
        lax.all_to_all(grad_qh, "seq", split_axis=1, concat_axis=2, tiled=True),
        lax.all_to_all(grad_kh, "seq", split_axis=1, concat_axis=2, tiled=True),
        lax.all_to_all(grad_vh, "seq", split_axis=1, concat_axis=2, tiled=True),
    )
    grad_qkv = jnp.concatenate([grad_q, grad_k, grad_v], axis=2).reshape(row_count, 3 * attn_width)
    grad_w_qkv = matmul_tn(hidden1, grad_qkv)
    grad_b_qv = jnp.stack(
        [
            jnp.sum(grad_q.astype(jnp.float32), axis=(0, 1)),
            jnp.sum(grad_v.astype(jnp.float32), axis=(0, 1)),
        ]
    )
    grad_h1 = matmul_nt(grad_qkv, back_qkv).reshape(lat_dev, seq_loc, width)
    grad_tokens = (grad_resid1 + norm_back(grad_h1 * (1.0 + scale_attn), normed1, inv1)).astype(
        jnp.bfloat16
    )
    grad_mods = jnp.stack(
        [
            token_sums(grad_h1),
            token_sums(grad_h1 * normed1),
            token_sums(grad_resid1 * attn_out),
            token_sums(grad_h2),
            token_sums(grad_h2 * normed2),
            token_sums(grad_y * ff_out),
        ],
        axis=1,
    )
    grad_mods_low = grad_mods.reshape(lat_dev, 6 * width).astype(jnp.bfloat16)
    grad_b_ada = jnp.sum(grad_mods_low.astype(jnp.float32), axis=0)
    grad_w_ada = lax.psum_scatter(
        matmul_tn(cond_act, grad_mods_low).astype(jnp.bfloat16),
        "fsdp",
        scatter_dimension=0,
        tiled=True,
    )
    grad_cond_act = matmul_nt(grad_mods_low, full_ada)
    grad_cond_part = grad_cond_act * cond_sig * (1.0 + condition * (1.0 - cond_sig))
    s_wqkv, s_bqv, s_wout, s_bout, s_wup, s_bup, s_wdown, s_bdown, s_bada = (
        lax.psum_scatter(grad_w_qkv, ("fsdp", "seq"), scatter_dimension=0, tiled=True),
        lax.psum_scatter(grad_b_qv, ("fsdp", "seq"), scatter_dimension=1, tiled=True),
        lax.psum_scatter(grad_w_out, ("fsdp", "seq"), scatter_dimension=0, tiled=True),
        lax.psum_scatter(grad_b_out, ("fsdp", "seq"), scatter_dimension=0, tiled=True),
        lax.psum_scatter(grad_w_up, ("fsdp", "seq"), scatter_dimension=0, tiled=True),
        lax.psum_scatter(grad_b_up, ("fsdp", "seq"), scatter_dimension=0, tiled=True),
        lax.psum_scatter(grad_w_down, ("fsdp", "seq"), scatter_dimension=0, tiled=True),
        lax.psum_scatter(grad_b_down, ("fsdp", "seq"), scatter_dimension=0, tiled=True),
        lax.psum_scatter(grad_b_ada, ("fsdp", "seq"), scatter_dimension=0, tiled=True),
    )
    t_wqkv, t_bqv, t_wout, t_bout, t_wup, t_bup, t_wdown, t_bdown, t_bada = (
        lax.all_gather(s_wqkv.astype(jnp.bfloat16), "seq", axis=0, tiled=True).astype(s_wqkv.dtype),
        lax.all_gather(s_bqv.astype(jnp.bfloat16), "seq", axis=1, tiled=True).astype(s_bqv.dtype),
        lax.all_gather(s_wout.astype(jnp.bfloat16), "seq", axis=0, tiled=True).astype(s_wout.dtype),
        lax.all_gather(s_bout.astype(jnp.bfloat16), "seq", axis=0, tiled=True).astype(s_bout.dtype),
        lax.all_gather(s_wup.astype(jnp.bfloat16), "seq", axis=0, tiled=True).astype(s_wup.dtype),
        lax.all_gather(s_bup.astype(jnp.bfloat16), "seq", axis=0, tiled=True).astype(s_bup.dtype),
        lax.all_gather(s_wdown.astype(jnp.bfloat16), "seq", axis=0, tiled=True).astype(
            s_wdown.dtype
        ),
        lax.all_gather(s_bdown.astype(jnp.bfloat16), "seq", axis=0, tiled=True).astype(
            s_bdown.dtype
        ),
        lax.all_gather(s_bada.astype(jnp.bfloat16), "seq", axis=0, tiled=True).astype(s_bada.dtype),
    )
    t_wada, t_cond = (
        lax.psum(grad_w_ada, "seq").astype(jnp.float32),
        lax.psum(grad_cond_part.astype(jnp.bfloat16), "seq").astype(jnp.float32),
    )
    return (
        output,
        grad_tokens,
        t_cond,
        t_wada,
        t_bada,
        t_wqkv,
        t_bqv,
        t_wout,
        t_bout,
        t_wup,
        t_bup,
        t_wdown,
        t_bdown,
    )


def solution(mesh):
    in_specs = (
        P("fsdp", "seq", None),
        P("fsdp", None),
        P("fsdp", None),
        P("fsdp"),
        P("fsdp", None),
        P(None, "fsdp"),
        P("fsdp", None),
        P("fsdp"),
        P("fsdp", None),
        P("fsdp"),
        P("fsdp", None),
        P("fsdp"),
        P("fsdp", "seq", None),
    )
    out_specs = (
        P("fsdp", "seq", None),
        P("fsdp", "seq", None),
        P("fsdp", None),
        P("fsdp", None),
        P("fsdp"),
        P("fsdp", None),
        P(None, "fsdp"),
        P("fsdp", None),
        P("fsdp"),
        P("fsdp", None),
        P("fsdp"),
        P("fsdp", None),
        P("fsdp"),
    )
    return jax.shard_map(local, mesh=mesh, in_specs=in_specs, out_specs=out_specs, check_vma=False)
```

profile of v0, /device:TPU:0, one launch (start us, length us, event | category | flops | bytes accessed | tf_op | source)
XLA Modules:
  0.0 1821.1 jit_solution(10421692875912982630)
XLA Ops:
  13.2 22.8 %all-gather = bf16[8,144,2]{1,2,0:T(2,128)(2,1)S(1)} all-gather(bf16[1,144,2]{1,2,0:T(2,128)(2,1)S(1)} %bitcast.233), channel_id=1, replica_groups=mesh['fsdp'=8,'seq'=4] {'fsdp'}, dimensions={0}, use_global_device_ids=true | all-gather | bytes 5184 | tf_op jit(solution)/shard_map/all_gather | solution.py:128
  37.1 36.0 %all-reduce.20 = (bf16[6912]{0:T(1024)(128)(2,1)S(1)}, bf16[1152]{0:T(1024)(128)(2,1)}, bf16[1152]{0:T(1024)(128)(2,1)}, bf16[4608]{0:T(1024)(128)(2,1)}) all-reduce(bf16[6912]{0:T(1024)(128)(2,1)S(1)} %dynamic-update-slice, bf16[1152]{0:T(1024)(128)(2,1)S(1)} %dynamic-update-slice.1, ...), channel_id=1, replica_groups=mesh['fsdp'=8,'seq'=4] {'fsdp'}, use_global_device_ids=true, to_apply=%add | all-reduce | flops 13824 | bytes 55296
  73.7 156.8 %all-gather.13.cloned.1.call-done = bf16[1152,6912]{1,0:T(8,128)(2,1)} async-done(((bf16[144,6912]{1,0:T(8,128)(2,1)}), bf16[1152,6912]{1,0:T(8,128)(2,1)}) %all-gather.13.cloned.1.call-update) | async-done | bytes 15925264 | tf_op jit(solution)/shard_map/all_gather | solution.py:140
  230.4 7.7 convolution_reduce_fusion
  238.9 111.1 %all-gather.15.cloned.1.call-done = bf16[1152,3456]{1,0:T(8,128)(2,1)} async-done(((bf16[144,3456]{1,0:T(8,128)(2,1)}), bf16[1152,3456]{1,0:T(8,128)(2,1)}) %all-gather.15.cloned.1.call-update) | async-done | bytes 7962640 | tf_op jit(solution)/shard_map/all_gather | solution.py:127
  350.0 6.0 fusion.74
  360.4 6.2 reduce.42
  373.3 6.2 reduce.43
  387.6 6.2 reduce.44
  394.8 4.6 all-to-all-start.2
  402.5 6.4 all-to-all-done.2
  412.1 8.5 multiply_reduce_fusion
  420.6 8.6 exponential_reduce_fusion
  429.2 9.6 convolution_convert_fusion.4
  438.8 4.2 copy.133
  443.0 6.5 reduce.45
  452.9 4.1 all-to-all-start.3
  458.3 8.3 all-to-all-done.3
  480.3 77.8 %all-gather.19.cloned.1.call-done = bf16[1152,4608]{1,0:T(8,128)(2,1)} async-done(((bf16[144,4608]{1,0:T(8,128)(2,1)}), bf16[1152,4608]{1,0:T(8,128)(2,1)}) %all-gather.19.cloned.1.call-update) | async-done | bytes 10616848 | tf_op jit(solution)/shard_map/all_gather | solution.py:131
  558.1 6.2 convolution_add_fusion
  566.7 9.3 fusion.52
  577.3 133.2 %all-gather.21.cloned.1.call-done = bf16[4608,1152]{1,0:T(8,128)(2,1)} async-done(((bf16[576,1152]{1,0:T(8,128)(2,1)}), bf16[4608,1152]{1,0:T(8,128)(2,1)}) %all-gather.21.cloned.1.call-update) | async-done | bytes 10616848 | tf_op jit(solution)/shard_map/all_gather | solution.py:133
  710.4 9.1 fusion.85
  719.7 9.7 fusion.34
  730.2 10.7 fusion.18
  747.5 8.1 reduce.46
  757.6 13.9 all_to_all.129
  780.5 9.7 convolution_convert_fusion.1
  790.1 4.5 copy.148
  794.7 7.4 reduce.47
  805.5 4.4 all-to-all-start.7
  811.3 11.2 multiply_convert_fusion.1
  826.1 4.5 copy.144
  830.6 7.4 reduce.48
  841.4 4.6 all-to-all-start.6
  846.0 5.4 convolution_convert_fusion.3
  854.3 6.5 reduce.49
  862.7 4.2 all-to-all-start.5
  870.0 4.2 reshape.484
  879.2 4.1 reshape.486
  883.2 4.6 copy.145
  890.5 4.1 reshape.488
  894.6 4.6 copy.141
  901.0 7.3 fusion.29
  914.8 6.6 multiply_convert_fusion
  921.5 4.8 fusion.57
  926.4 9.3 fusion.39
  935.8 8.1 fusion.43
  943.9 577.5 %fusion.80 = (f32[48,3456]{1,0:T(8,128)S(1)}, f32[48,1152]{1,0:T(8,128)S(1)}, f32[40,4608]{1,0:T(8,128)S(1)}) fusion(f32[1152,3456]{1,0:T(8,128)} %fusion.43, f32[1152,1152]{1,0:T(8,128)} %fusion.57, f32[1152,4608]{1,0:T(8,128)} %fusion.39), kind=kCustom, calls=%all-reduce-scatter.3 | all-reduce-scatter fusion | flops 12976130 | bytes 44089344
  1524.2 35.0 %collective-permute-start.17 = (bf16[40,4608]{1,0:T(8,128)(2,1)}, bf16[40,4608]{1,0:T(8,128)(2,1)}, u32[]{:S(2)}, u32[]{:S(2)}) collective-permute-start(bf16[40,4608]{1,0:T(8,128)(2,1)} %convert.54), channel_id=1, source_target_pairs={{0,2},{1,3},{2,4},{3,5},{4,6},{5,7},{6,8},{7,9},{8,10},{9,11},{10,... | collective-permute-start | bytes 1105928
  1563.8 9.4 collective-permute-done.19
  1573.1 16.8 concatenate.12
  1595.9 6.9 collective-permute-start.14
  1605.0 5.8 collective-permute-start.12
  1623.1 9.8 fusion.11
  1632.9 39.3 %all-reduce.19 = (bf16[6912]{0:T(1024)(128)(2,1)S(1)}, bf16[2,1152]{1,0:T(2,128)(2,1)S(1)}, bf16[1152]{0:T(1024)(128)(2,1)S(1)}, bf16[4608]{0:T(1024)(128)(2,1)S(1)}, bf16[1152]{0:T(1024)(128)(2,1)S(1)}) all-reduce(bf16[6912]{0:T(1024)(128)(2,1)S(1)} %copy-done.22, ...), channel_id=3, replica_groups=mesh['fsdp'=8,'seq'=4] {'fsdp','seq'}, use_global_device_ids=true, to_apply=%region_20.21.clone | all-reduce | flops 16128 | bytes 82944
  1672.3 4.0 collective-permute-start.5
  1676.3 4.9 collective-permute-start.11
  1686.6 5.0 all-gather.2
  1697.5 7.8 all-reduce.21
  1714.4 5.3 concatenate.11
  1728.7 28.5 %all-gather.3 = bf16[4,36,1152]{2,1,0:T(8,128)(2,1)S(1)} all-gather(bf16[1,36,1152]{2,1,0:T(8,128)(2,1)S(1)} %fusion.60), channel_id=1, replica_groups=mesh['fsdp'=8,'seq'=4] {'seq'}, dimensions={0}, use_global_device_ids=true | all-gather | bytes 414720 | tf_op jit(solution)/shard_map/all_gather | solution.py:262
  1758.1 33.7 %concatenate.10 = bf16[420,3456]{1,0:T(8,128)(2,1)} concatenate(bf16[36,3456]{1,0:T(8,128)(2,1)} %collective-permute-done.7, bf16[48,3456]{1,0:T(8,128)(2,1)S(1)} %collective-permute-done.6, bf16[48,3456]{1,0:T(8,128)(2,1)} %copy-done.18, bf16[48,3456]{1,0:T(8,128)(2,1)} %collective-permute-done.4, bf16[48,3456]{1,0:T(8,128)(2,1)} %collective-permute-done.3, ...), dimensions={0} | concatenate | bytes 6137856
  1792.9 10.3 all-gather.1
  (323 shorter events, 176.6 us)
Async XLA Ops:
  7.2 223.3 %all-gather.13.cloned.1.call-start = ((), (), s32[]{:S(2)}) async-start(), calls=%async_computation.10 | async-start | bytes 17915904 | tf_op jit(solution)/shard_map/all_gather | solution.py:140
  7.9 28.2 %copy-start.57 = (bf16[144]{0:T(256)(128)(2,1)S(1)}, bf16[144]{0:T(256)(128)(2,1)}, u32[]{:S(2)}) copy-start(bf16[144]{0:T(256)(128)(2,1)} %param.20) | copy-start | bytes 868
  7.9 28.4 %copy-start.58 = (bf16[144]{0:T(256)(128)(2,1)S(1)}, bf16[144]{0:T(256)(128)(2,1)}, u32[]{:S(2)}) copy-start(bf16[144]{0:T(256)(128)(2,1)} %param.24) | copy-start | bytes 868
  8.0 28.7 %copy-start.54 = (bf16[864]{0:T(1024)(128)(2,1)S(1)}, bf16[864]{0:T(1024)(128)(2,1)}, u32[]{:S(2)}) copy-start(bf16[864]{0:T(1024)(128)(2,1)} %param.16) | copy-start | bytes 5188
  8.0 28.9 %copy-start.55 = (bf16[576]{0:T(1024)(128)(2,1)S(1)}, bf16[576]{0:T(1024)(128)(2,1)}, u32[]{:S(2)}) copy-start(bf16[576]{0:T(1024)(128)(2,1)} %param.22) | copy-start | bytes 3460
  8.0 65.2 %copy-start.1 = (bf16[1,256,1152]{2,1,0:T(8,128)(2,1)S(1)}, bf16[1,256,1152]{2,1,0:T(8,128)(2,1)}, u32[]{:S(2)}) copy-start(bf16[1,256,1152]{2,1,0:T(8,128)(2,1)} %param.13) | copy-start | bytes 1769476
  8.0 342.0 %all-gather.15.cloned.1.call-start = ((), (), s32[]{:S(2)}) async-start(), calls=%async_computation.11 | async-start | bytes 8957952 | tf_op jit(solution)/shard_map/all_gather | solution.py:127
  8.7 466.2 %all-gather.17.cloned.1.call-start = ((), (), s32[]{:S(2)}) async-start(), calls=%async_computation.12 | async-start | bytes 2985984 | tf_op jit(solution)/shard_map/all_gather | solution.py:129
  9.5 221.0 %copy-start.28 = (f32[1,1152]{1,0:T(1,128)S(1)}, f32[1,1152]{1,0:T(1,128)}, u32[]{:S(2)}) copy-start(f32[1,1152]{1,0:T(1,128)} %param.14) | copy-start | bytes 13828
  9.5 548.6 %all-gather.19.cloned.1.call-start = ((), (), s32[]{:S(2)}) async-start(), calls=%async_computation.13 | async-start | bytes 11943936 | tf_op jit(solution)/shard_map/all_gather | solution.py:131
  10.1 700.4 %all-gather.21.cloned.1.call-start = ((), (), s32[]{:S(2)}) async-start(), calls=%async_computation.14 | async-start | bytes 11943936 | tf_op jit(solution)/shard_map/all_gather | solution.py:133
  73.3 276.6 %copy-start.36 = (f32[256]{0:T(256)}, f32[256]{0:T(256)S(1)}, u32[]{:S(2)}) copy-start(f32[256]{0:T(256)S(1)} %broadcast_multiply_fusion.5) | copy-start | bytes 3076
  73.6 276.3 %copy-start.43 = (f32[256]{0:T(256)}, f32[256]{0:T(256)S(1)}, u32[]{:S(2)}) copy-start(f32[256]{0:T(256)S(1)} %add_rsqrt_fusion.1) | copy-start | bytes 3076
  238.9 117.1 %copy-start.25 = (f32[1152]{0:T(1024)}, f32[1152]{0:T(1024)S(1)}, u32[]{:S(2)}) copy-start(f32[1152]{0:T(1024)S(1)} %get-tuple-element.76) | copy-start | bytes 13828
  367.5 13.2 all-to-all-start
  380.6 14.1 all-to-all-start.1
  394.8 14.1 all-to-all-start.2
  400.9 28.3 %copy-start.10 = (bf16[1024,4,72]{0,2,1:T(8,128)(2,1)}, bf16[1024,4,72]{0,2,1:T(8,128)(2,1)S(1)}, u32[]{:S(2)}) copy-start(bf16[1024,4,72]{0,2,1:T(8,128)(2,1)S(1)} %reshape.384) | copy-start | bytes 1769476
  442.9 14.2 copy-start.50
  443.0 14.8 copy-start.46
  452.9 13.7 all-to-all-start.3
  457.1 1161.1 %reduce-scatter.12.cloned.1.call-start = ((), (), s32[]{:S(2)}) async-start(), calls=%async_computation.17 | async-start | bytes 21897216 | tf_op jit(solution)/shard_map/reduce_scatter | solution.py:255
  719.6 10.5 copy-start.3
  719.6 10.5 copy-start.15
  719.6 10.5 copy-start.17
  719.6 10.5 copy-start.27
  719.6 10.5 copy-start.32
  730.2 11.7 copy-start.6
  805.5 35.9 %all-to-all-start.7 = ((bf16[4,2,36864]{2,1,0:T(2,128)(2,1)}), bf16[4,2,36864]{2,1,0:T(2,128)(2,1)}, u32[]{:S(2)}, u32[]{:S(2)}) async-start(bf16[4,2,36864]{2,1,0:T(2,128)(2,1)} %reshape.483), calls=%async_computation.7 | async-start | bytes 1179648 | tf_op jit(solution)/shard_map/all_to_all | solution.py:213
  841.4 21.4 %all-to-all-start.6 = ((bf16[4,2,36864]{2,1,0:T(2,128)(2,1)}), bf16[4,2,36864]{2,1,0:T(2,128)(2,1)}, u32[]{:S(2)}, u32[]{:S(2)}) async-start(bf16[4,2,36864]{2,1,0:T(2,128)(2,1)} %reshape.485), calls=%async_computation.6 | async-start | bytes 1179648 | tf_op jit(solution)/shard_map/all_to_all | solution.py:212
  854.3 12.7 copy-start.29
  854.3 13.3 copy-start.53
  854.3 13.9 copy-start.42
  854.3 14.5 copy-start.51
  854.3 15.1 copy-start.52
  862.7 27.7 %all-to-all-start.5 = ((bf16[4,2,36864]{2,1,0:T(2,128)(2,1)}), bf16[4,2,36864]{2,1,0:T(2,128)(2,1)}, u32[]{:S(2)}, u32[]{:S(2)}) async-start(bf16[4,2,36864]{2,1,0:T(2,128)(2,1)} %reshape.487), calls=%async_computation.5 | async-start | bytes 1179648 | tf_op jit(solution)/shard_map/all_to_all | solution.py:211
  866.9 852.7 %reduce-scatter.10.cloned.1.call-start = ((), (), s32[]{:S(2)}) async-start(), calls=%async_computation.15 | async-start | bytes 17915904 | tf_op jit(solution)/shard_map/reduce_scatter | solution.py:240
  921.4 883.1 %all-gather.25.cloned.1.call-start = ((), (), s32[]{:S(2)}) async-start(), calls=%async_computation.19 | async-start | bytes 1843200 | tf_op jit(solution)/shard_map/all_gather | solution.py:264
  1522.2 50.9 %collective-permute-start.18 = (bf16[40,4608]{1,0:T(8,128)(2,1)}, bf16[40,4608]{1,0:T(8,128)(2,1)}, u32[]{:S(2)}, u32[]{:S(2)}) collective-permute-start(bf16[40,4608]{1,0:T(8,128)(2,1)} %convert.54), channel_id=1, source_target_pairs={{0,3},{1,4},{2,5},{3,6},{4,7},{5,8},{6,9},{7,10},{8,11},{9,12},{10... | collective-permute-start | bytes 1105928
  1524.2 48.9 %collective-permute-start.17 = (bf16[40,4608]{1,0:T(8,128)(2,1)}, bf16[40,4608]{1,0:T(8,128)(2,1)}, u32[]{:S(2)}, u32[]{:S(2)}) collective-permute-start(bf16[40,4608]{1,0:T(8,128)(2,1)} %convert.54), channel_id=1, source_target_pairs={{0,2},{1,3},{2,4},{3,5},{4,6},{5,7},{6,8},{7,9},{8,10},{9,11},{10,... | collective-permute-start | bytes 1105928
  1559.2 13.9 collective-permute-start.16
  1562.3 10.8 collective-permute-start.19
  1563.7 28.1 %copy-start.59 = (u32[32]{0:T(128)S(1)}, u32[32]{0:T(128)}, u32[]{:S(2)}) copy-start(u32[32]{0:T(128)} %constant.92) | copy-start | bytes 388
  1589.9 20.8 %copy-start.19 = (bf16[1,6,1152]{2,1,0:T(8,128)(2,1)S(1)}, bf16[1,6,1152]{2,1,0:T(8,128)(2,1)}, u32[]{:S(2)}) copy-start(bf16[1,6,1152]{2,1,0:T(8,128)(2,1)} %stack.36) | copy-start | bytes 41476
  1591.8 215.4 %all-gather.23.cloned.1.call-start = ((), (), s32[]{:S(2)}) async-start(), calls=%async_computation.18 | async-start | bytes 1658880 | tf_op jit(solution)/shard_map/all_gather | solution.py:266
  1595.2 24.9 %copy-start.38 = (f32[256]{0:T(256)S(1)}, f32[256]{0:T(256)}, u32[]{:S(2)}) copy-start(f32[256]{0:T(256)} %copy-done.36) | copy-start | bytes 3076
  1595.2 24.9 %copy-start.45 = (f32[256]{0:T(256)S(1)}, f32[256]{0:T(256)}, u32[]{:S(2)}) copy-start(f32[256]{0:T(256)} %copy-done.43) | copy-start | bytes 3076
  1595.9 80.4 %collective-permute-start.14 = (bf16[48,1152]{1,0:T(8,128)(2,1)S(1)}, bf16[48,1152]{1,0:T(8,128)(2,1)S(1)}, u32[]{:S(2)}, u32[]{:S(2)}) collective-permute-start(bf16[48,1152]{1,0:T(8,128)(2,1)S(1)} %convert.56), channel_id=1, source_target_pairs={{0,7},{1,8},{2,9},{3,10},{4,11},{5,12},{6,13},{7,14},{8,15},{9,16}... | collective-permute-start | bytes 331784
  1602.8 78.5 %collective-permute-start.13 = (bf16[48,1152]{1,0:T(8,128)(2,1)S(1)}, bf16[48,1152]{1,0:T(8,128)(2,1)}, u32[]{:S(2)}, u32[]{:S(2)}) collective-permute-start(bf16[48,1152]{1,0:T(8,128)(2,1)S(1)} %convert.56), channel_id=1, source_target_pairs={{0,6},{1,7},{2,8},{3,9},{4,10},{5,11},{6,12},{7,13},{8,14},{9,15},... | collective-permute-start | bytes 331784
  1605.0 77.6 %collective-permute-start.12 = (bf16[48,1152]{1,0:T(8,128)(2,1)S(1)}, bf16[48,1152]{1,0:T(8,128)(2,1)}, u32[]{:S(2)}, u32[]{:S(2)}) collective-permute-start(bf16[48,1152]{1,0:T(8,128)(2,1)S(1)} %convert.56), channel_id=1, source_target_pairs={{0,5},{1,6},{2,7},{3,8},{4,9},{5,10},{6,11},{7,12},{8,13},{9,14},{... | collective-permute-start | bytes 331784
  1611.9 111.1 %collective-permute-start.6 = (bf16[48,3456]{1,0:T(8,128)(2,1)S(1)}, bf16[48,3456]{1,0:T(8,128)(2,1)S(1)}, u32[]{:S(2)}, u32[]{:S(2)}) collective-permute-start(bf16[48,3456]{1,0:T(8,128)(2,1)S(1)} %convert.55), channel_id=1, source_target_pairs={{0,7},{1,8},{2,9},{3,10},{4,11},{5,12},{6,13},{7,14},{8,15},{9,16}... | collective-permute-start | bytes 995336
  1613.3 59.0 %collective-permute-start.15 = (bf16[36,1152]{1,0:T(8,128)(2,1)}, bf16[36,1152]{1,0:T(8,128)(2,1)S(1)}, u32[]{:S(2)}, u32[]{:S(2)}) collective-permute-start(bf16[36,1152]{1,0:T(8,128)(2,1)} %slice.57), channel_id=1, source_target_pairs={{0,8},{1,9},{2,10},{3,11},{4,12},{5,13},{6,14},{7,15},{8,16},{9,17... | collective-permute-start | bytes 248840
  1620.1 190.2 %all-reduce.25.cloned.1.call-start = ((), (), s32[]{:S(2)}) async-start(), calls=%async_computation.16 | async-start | bytes 3981312 | tf_op jit(solution)/shard_map/psum | solution.py:275
  1672.3 54.3 %collective-permute-start.5 = (bf16[48,3456]{1,0:T(8,128)(2,1)S(1)}, bf16[48,3456]{1,0:T(8,128)(2,1)S(1)}, u32[]{:S(2)}, u32[]{:S(2)}) collective-permute-start(bf16[48,3456]{1,0:T(8,128)(2,1)S(1)} %convert.55), channel_id=1, source_target_pairs={{0,6},{1,7},{2,8},{3,9},{4,10},{5,11},{6,12},{7,13},{8,14},{9,15},... | collective-permute-start | bytes 995336
  1676.3 15.3 collective-permute-start.11
  1681.3 12.8 collective-permute-start.10
  1682.6 37.1 %collective-permute-start.7 = (bf16[36,3456]{1,0:T(8,128)(2,1)}, bf16[36,3456]{1,0:T(8,128)(2,1)}, u32[]{:S(2)}, u32[]{:S(2)}) collective-permute-start(bf16[36,3456]{1,0:T(8,128)(2,1)} %slice.56), channel_id=1, source_target_pairs={{0,8},{1,9},{2,10},{3,11},{4,12},{5,13},{6,14},{7,15},{8,16},{9,17... | collective-permute-start | bytes 746504
  1691.6 17.2 collective-permute-start.9
  1694.1 16.8 collective-permute-start.8
  1708.9 49.2 %collective-permute-start.4 = (bf16[48,3456]{1,0:T(8,128)(2,1)S(1)}, bf16[48,3456]{1,0:T(8,128)(2,1)}, u32[]{:S(2)}, u32[]{:S(2)}) collective-permute-start(bf16[48,3456]{1,0:T(8,128)(2,1)S(1)} %convert.55), channel_id=1, source_target_pairs={{0,5},{1,6},{2,7},{3,8},{4,9},{5,10},{6,11},{7,12},{8,13},{9,14},{... | collective-permute-start | bytes 995336
  1711.5 46.6 %collective-permute-start.3 = (bf16[48,3456]{1,0:T(8,128)(2,1)S(1)}, bf16[48,3456]{1,0:T(8,128)(2,1)}, u32[]{:S(2)}, u32[]{:S(2)}) collective-permute-start(bf16[48,3456]{1,0:T(8,128)(2,1)S(1)} %convert.55), channel_id=1, source_target_pairs={{0,4},{1,5},{2,6},{3,7},{4,8},{5,9},{6,10},{7,11},{8,12},{9,13},{1... | collective-permute-start | bytes 995336
  1719.7 38.4 %collective-permute-start.2 = (bf16[48,3456]{1,0:T(8,128)(2,1)S(1)}, bf16[48,3456]{1,0:T(8,128)(2,1)S(1)}, u32[]{:S(2)}, u32[]{:S(2)}) collective-permute-start(bf16[48,3456]{1,0:T(8,128)(2,1)S(1)} %convert.55), channel_id=1, source_target_pairs={{0,3},{1,4},{2,5},{3,6},{4,7},{5,8},{6,9},{7,10},{8,11},{9,12},{10... | collective-permute-start | bytes 995336
  1723.0 35.1 %collective-permute-start.1 = (bf16[48,3456]{1,0:T(8,128)(2,1)S(1)}, bf16[48,3456]{1,0:T(8,128)(2,1)}, u32[]{:S(2)}, u32[]{:S(2)}) collective-permute-start(bf16[48,3456]{1,0:T(8,128)(2,1)S(1)} %convert.55), channel_id=1, source_target_pairs={{0,2},{1,3},{2,4},{3,5},{4,6},{5,7},{6,8},{7,9},{8,10},{9,11},{10,... | collective-permute-start | bytes 995336
  1726.6 31.5 %collective-permute-start = (bf16[48,3456]{1,0:T(8,128)(2,1)S(1)}, bf16[48,3456]{1,0:T(8,128)(2,1)}, u32[]{:S(2)}, u32[]{:S(2)}) collective-permute-start(bf16[48,3456]{1,0:T(8,128)(2,1)S(1)} %convert.55), channel_id=1, source_target_pairs={{0,1},{1,2},{2,3},{3,4},{4,5},{5,6},{6,7},{7,8},{8,9},{9,10},{10,1... | collective-permute-start | bytes 995336
  (34 other events, 215.7 us)
Sparse Core Ops, SparseCore 0:
  10.2 220.2 all-gather.12
  232.6 117.2 all-gather.14
  352.1 53.1 all-gather.16
  407.4 150.6 all-gather.18
  560.1 150.2 all-gather.20
  716.7 223.8 reduce-scatter.11
  944.5 459.7 reduce-scatter.9
  1591.9 24.1 all-gather.24
  1620.2 22.7 all-gather.22
  1719.8 62.0 all-reduce.24
where the time goes:
time: 1840 us; the launch traced here: 1820 us
  blocking collectives  741 us (40%)
  waiting for transfers between devices  506 us (28%)
  local copies, waits for them, and re-layouts  183 us (10%)
  matrix products  152 us (8%)
  starting transfers between devices  123 us (7%)
  other arithmetic  95.9 us (5%)
  between operations  19.6 us (1%)
    unnamed x3, blocking collectives  653 us
    all_gather x1, waiting for transfers between devices, local(): full_ada = lax.all_gather(w_ada, 'fsdp', axis=0, tiled=True)  157 us
    all_gather x1, waiting for transfers between devices, local(): lax.all_gather(w_down, 'fsdp', axis=0, tiled=True)  133 us
    unnamed x177, local copies, waits for them, and re-layouts  114 us
    all_gather x1, waiting for transfers between devices, local(): lax.all_gather(w_qkv, 'fsdp', axis=0, tiled=True)  111 us
    unnamed x20, starting transfers between devices  93.5 us
    all_gather x1, waiting for transfers between devices, local(): lax.all_gather(w_up, 'fsdp', axis=0, tiled=True)  77.8 us
    unnamed x11, other arithmetic  55.1 us
  transfers between devices with their start and end apart: 37, of which 8 were waited for; matrix products, arithmetic and copies ran while one was open for 54% of the time, Pallas kernels for 0%

commit v1 on v0

v1 whole, which is shorter than its diff:
```python
import functools

import jax
import jax.numpy as jnp
from jax import lax
from jax.experimental import pallas as pl
from jax.experimental.pallas import tpu as pltpu
from jax.sharding import PartitionSpec as P

HD = 72
EPSILON = 1e-06
GELU_C = 0.7978845608028654
SCALE = HD**-0.5
BF = jnp.bfloat16
F32 = jnp.float32
VMEM_LIMIT = 60 * 1024 * 1024


def dot(left, right):
    return jnp.dot(left, right, preferred_element_type=F32)


def dot_nt(left, right):
    return lax.dot_general(left, right, (((1,), (1,)), ((), ())), preferred_element_type=F32)


def dot_tn(left, right):
    return lax.dot_general(left, right, (((0,), (0,)), ((), ())), preferred_element_type=F32)


def rows_of(block, size):
    return pl.ds(pl.multiple_of(block * size, size), size)


def layer_norm(values):
    mean_val = jnp.mean(values, axis=-1, keepdims=True)
    centred = values - mean_val
    inv_std = lax.rsqrt(jnp.mean(centred * centred, axis=-1, keepdims=True) + EPSILON)
    return (centred * inv_std, inv_std)


def norm_back(grad_norm, normed, inv_std):
    first = jnp.mean(grad_norm, axis=-1, keepdims=True)
    second = jnp.mean(grad_norm * normed, axis=-1, keepdims=True)
    return inv_std * (grad_norm - first - normed * second)


def attn_kernel(heads, block, h_ref, w_ref, b_ref, wo_ref, part_ref, qkv_ref, mix_ref, lse_ref):
    total = h_ref.shape[0]
    steps = total // block

    def project(step, carry):
        at = rows_of(step, block)
        qkv = (dot(h_ref[at, :], w_ref[...]) + b_ref[...]).astype(BF)
        for j in range(3 * heads):
            qkv_ref[j, at, :] = qkv[:, j * HD : (j + 1) * HD]
        return carry

    lax.fori_loop(0, steps, project, 0)

    def attend(step, carry):
        at = rows_of(step, block)
        mixed, lses = [], []
        for h in range(heads):
            scores = dot_nt(qkv_ref[h, at, :], qkv_ref[heads + h, :, :])
            highest = jnp.max(scores, axis=-1, keepdims=True)
            weights = jnp.exp((scores - highest) * SCALE)
            total_w = jnp.sum(weights, axis=-1, keepdims=True)
            probs = (weights * (1.0 / total_w)).astype(BF)
            mixed.append(dot(probs, qkv_ref[2 * heads + h, :, :]).astype(BF))
            lses.append(highest * SCALE + jnp.log(total_w))
        mix = jnp.concatenate(mixed, axis=1)
        mix_ref[at, :] = mix
        lse_ref[at, :] = jnp.concatenate(lses, axis=1)
        part_ref[at, :] = dot(mix, wo_ref[...]).astype(BF)
        return carry

    lax.fori_loop(0, steps, attend, 0)


def attn_forward(hidden, w_qkv, bias, w_out):
    total, width = hidden.shape
    inner = w_out.shape[0]
    heads = inner // HD
    vmem = pl.BlockSpec(memory_space=pltpu.VMEM)
    return pl.pallas_call(
        functools.partial(attn_kernel, heads, 256),
        out_shape=(
            jax.ShapeDtypeStruct((total, width), BF),
            jax.ShapeDtypeStruct((3 * heads, total, HD), BF),
            jax.ShapeDtypeStruct((total, inner), BF),
            jax.ShapeDtypeStruct((total, heads), F32),
        ),
        in_specs=[vmem] * 4,
        out_specs=(vmem,) * 4,
        compiler_params=pltpu.CompilerParams(vmem_limit_bytes=VMEM_LIMIT),
        cost_estimate=pl.CostEstimate(
            flops=2 * total * width * inner * 4 + 4 * total * total * heads * 128,
            bytes_accessed=2 * (2 * total * width + 4 * width * inner + 5 * total * inner),
            transcendentals=heads * total * total,
        ),
        name="attn_forward",
    )(hidden, w_qkv, bias, w_out)


def attn_back_kernel(
    heads, block, ga_ref, h_ref, w_ref, wo_ref, qkv_ref, mix_ref, lse_ref,
    gh_ref, gw_ref, gwo_ref, gb_ref, gqkv_ref, gk_acc, gv_acc,
):
    total, width = h_ref.shape
    inner = wo_ref.shape[0]
    steps = total // block
    gk_acc[...] = jnp.zeros_like(gk_acc)
    gv_acc[...] = jnp.zeros_like(gv_acc)

    def attend(step, carry):
        at = rows_of(step, block)
        grad_mix = dot_nt(ga_ref[at, :], wo_ref[...]).astype(BF)
        mix = mix_ref[at, :]
        lse = lse_ref[at, :]
        grads = []
        for h in range(heads):
            here = slice(h * HD, (h + 1) * HD)
            gm = grad_mix[:, here]
            query = qkv_ref[h, at, :]
            key = qkv_ref[heads + h, :, :]
            scores = dot_nt(query, key)
            probs = jnp.exp(scores * SCALE - lse[:, h : h + 1])
            delta = jnp.sum(gm.astype(F32) * mix[:, here].astype(F32), axis=-1, keepdims=True)
            grad_p = dot_nt(gm, qkv_ref[2 * heads + h, :, :])
            grad_s = (probs * (grad_p - delta) * SCALE).astype(BF)
            grads.append(dot(grad_s, key).astype(BF))
            gk_acc[h] += dot_tn(grad_s, query)
            gv_acc[h] += dot_tn(probs.astype(BF), gm)
        gqkv_ref[at, :inner] = jnp.concatenate(grads, axis=1)
        return carry

    lax.fori_loop(0, steps, attend, 0)
    gqkv_ref[:, inner : 2 * inner] = jnp.concatenate(
        [gk_acc[h].astype(BF) for h in range(heads)], axis=1
    )
    gqkv_ref[:, 2 * inner :] = jnp.concatenate(
        [gv_acc[h].astype(BF) for h in range(heads)], axis=1
    )

    def weight(step, carry):
        at = rows_of(step, 384)
        gw_ref[at, :] = dot_tn(h_ref[:, at], gqkv_ref[...]).astype(BF)
        return carry

    lax.fori_loop(0, width // 384, weight, 0)
    gwo_ref[...] = dot_tn(mix_ref[...], ga_ref[...]).astype(BF)

    def hidden(step, sums):
        at = rows_of(step, block)
        part = gqkv_ref[at, :]
        gh_ref[at, :] = dot_nt(part, w_ref[...]).astype(BF)
        return sums + jnp.sum(part.astype(F32), axis=0, keepdims=True)

    gb_ref[...] = lax.fori_loop(0, steps, hidden, jnp.zeros((1, 3 * inner), F32))


def attn_backward(grad_attn, hidden, w_qkv, w_out, qkv, mix, lse):
    total, width = hidden.shape
    inner = w_out.shape[0]
    heads = inner // HD
    vmem = pl.BlockSpec(memory_space=pltpu.VMEM)
    return pl.pallas_call(
        functools.partial(attn_back_kernel, heads, 256),
        out_shape=(
            jax.ShapeDtypeStruct((total, width), BF),
            jax.ShapeDtypeStruct((width, 3 * inner), BF),
            jax.ShapeDtypeStruct((inner, width), BF),
            jax.ShapeDtypeStruct((1, 3 * inner), F32),
        ),
        in_specs=[vmem] * 7,
        out_specs=(vmem,) * 4,
        scratch_shapes=[
            pltpu.VMEM((total, 3 * inner), BF),
            pltpu.VMEM((heads, total, HD), F32),
            pltpu.VMEM((heads, total, HD), F32),
        ],
        compiler_params=pltpu.CompilerParams(vmem_limit_bytes=VMEM_LIMIT),
        cost_estimate=pl.CostEstimate(
            flops=2 * total * width * inner * 8 + 10 * total * total * heads * 128,
            bytes_accessed=2 * (3 * total * width + 8 * width * inner + 5 * total * inner),
            transcendentals=heads * total * total,
        ),
        name="attn_backward",
    )(grad_attn, hidden, w_qkv, w_out, qkv, mix, lse)


def ff_kernel(
    block, h_ref, gf_ref, wu_ref, bu_ref, wd_ref,
    part_ref, gh_ref, gwu_ref, gwd_ref, gbu_ref, act_ref, gp_ref,
):
    total, width = h_ref.shape
    inner = wd_ref.shape[0]

    def rows(step, sums):
        at = rows_of(step, block)
        pre = dot(h_ref[at, :], wu_ref[...]) + bu_ref[...]
        square = pre * pre
        tanh_val = jnp.tanh(GELU_C * pre * (1.0 + 0.044715 * square))
        half = 0.5 * (1.0 + tanh_val)
        act = (pre * half).astype(BF)
        slope = half + 0.5 * GELU_C * pre * (1.0 - tanh_val * tanh_val) * (
            1.0 + 3.0 * 0.044715 * square
        )
        grad_pre = dot_nt(gf_ref[at, :], wd_ref[...]) * slope
        grad_low = grad_pre.astype(BF)
        act_ref[at, :] = act
        gp_ref[at, :] = grad_low
        gh_ref[at, :] = dot_nt(grad_low, wu_ref[...]).astype(BF)
        part_ref[at, :] = dot(act, wd_ref[...]).astype(BF)
        return sums + jnp.sum(grad_pre, axis=0, keepdims=True)

    gbu_ref[...] = lax.fori_loop(0, total // block, rows, jnp.zeros((1, inner), F32))

    def down(step, carry):
        at = rows_of(step, 384)
        gwd_ref[at, :] = dot_tn(act_ref[:, at], gf_ref[...]).astype(BF)
        return carry

    lax.fori_loop(0, inner // 384, down, 0)

    def up(step, carry):
        at = rows_of(step, 384)
        gwu_ref[at, :] = dot_tn(h_ref[:, at], gp_ref[...]).astype(BF)
        return carry

    lax.fori_loop(0, width // 384, up, 0)


def feed_forward(hidden, grad_ff, w_up, bias, w_down):
    total, width = hidden.shape
    inner = w_down.shape[0]
    vmem = pl.BlockSpec(memory_space=pltpu.VMEM)
    return pl.pallas_call(
        functools.partial(ff_kernel, 256),
        out_shape=(
            jax.ShapeDtypeStruct((total, width), BF),
            jax.ShapeDtypeStruct((total, width), BF),
            jax.ShapeDtypeStruct((width, inner), BF),
            jax.ShapeDtypeStruct((inner, width), BF),
            jax.ShapeDtypeStruct((1, inner), F32),
        ),
        in_specs=[vmem] * 5,
        out_specs=(vmem,) * 5,
        scratch_shapes=[pltpu.VMEM((total, inner), BF), pltpu.VMEM((total, inner), BF)],
        compiler_params=pltpu.CompilerParams(vmem_limit_bytes=VMEM_LIMIT),
        cost_estimate=pl.CostEstimate(
            flops=12 * total * width * inner,
            bytes_accessed=2 * (4 * total * width + 4 * width * inner),
            transcendentals=total * inner,
        ),
        name="feed_forward",
    )(hidden, grad_ff, w_up, bias, w_down)


def bits_of(count):
    found, bit = [], 1
    while bit < count:
        found.insert(0, bit)
        bit *= 2
    return found


def swap(values, count, bit):
    return lax.ppermute(values, "seq", [(i, i ^ bit) for i in range(count)])


def gather_seq(values, count):
    for bit in bits_of(count):
        values = jnp.concatenate([values, swap(values, count, bit)], axis=0)
    return values


def scatter_seq(values, count):
    for bit in reversed(bits_of(count)):
        half = values.shape[0] // 2
        got = swap(values[half:], count, bit)
        values = values[:half].astype(F32) + got.astype(F32)
        if bit != bits_of(count)[0]:
            values = values.astype(BF)
    return values


def local(n_f, n_s, tokens, condition, w_ada, b_ada, w_qkv, b_qv, w_out, b_out, w_up, b_up,
          w_down, b_down, grad_output):
    lat_dev, seq_loc, width = tokens.shape
    assert lat_dev == 1
    shard = w_qkv.shape[0]
    attn_width = w_qkv.shape[1] // 3
    ff_width = w_up.shape[1]
    inner = attn_width // n_s
    ff_q = ff_width // n_f // n_s
    mods_width = w_ada.shape[1]
    f_at = lax.axis_index("fsdp")
    s_at = lax.axis_index("seq")

    qkv_mine = lax.dynamic_index_in_dim(
        w_qkv.reshape(shard, 3, n_s, inner), s_at, 2, keepdims=False
    ).reshape(shard, 3 * inner)
    full_qkv = lax.all_gather(qkv_mine, "fsdp", axis=0, tiled=True)

    packed = jnp.concatenate(
        [condition.reshape(-1)]
        + [part.astype(F32).reshape(-1) for part in (b_qv, b_out, b_up, b_down)]
    )
    packed_all = lax.all_gather(packed, "fsdp", axis=0)
    sizes = [width, 2 * (attn_width // n_f), width // n_f, ff_width // n_f, width // n_f]
    parts, start = [], 0
    for size in sizes:
        parts.append(packed_all[:, start : start + size])
        start += size
    cond_all, bqv_all, bout_all, bup_all, bdown_all = parts
    full_bqv = bqv_all.reshape(n_f, 2, attn_width // n_f).transpose(1, 0, 2).reshape(2, n_s, inner)
    bqv_mine = lax.dynamic_index_in_dim(full_bqv, s_at, 1, keepdims=False)
    bias_qkv = jnp.concatenate([bqv_mine[0], jnp.zeros((inner,), F32), bqv_mine[1]])[None]
    full_bout = bout_all.reshape(1, width)
    full_bdown = bdown_all.reshape(1, width)
    bias_up = lax.dynamic_index_in_dim(
        bup_all.reshape(n_f, n_s, ff_q), s_at, 1, keepdims=False
    ).reshape(1, n_f * ff_q)

    act_all = (cond_all * jax.nn.sigmoid(cond_all)).astype(BF)
    act_rows = lax.dynamic_index_in_dim(
        act_all.reshape(n_f, n_f, shard), f_at, 1, keepdims=False
    )
    mods_part = dot(act_rows, w_ada)
    own_bias = lax.dynamic_update_slice(
        jnp.zeros((1, mods_width), F32), b_ada.astype(F32)[None], (0, f_at * b_ada.shape[0])
    )
    mods = lax.psum_scatter(mods_part + own_bias, "fsdp", scatter_dimension=0, tiled=True)
    shift_attn, scale_attn, gate_attn, shift_ff, scale_ff, gate_ff = [
        mods[:, i * width : (i + 1) * width] for i in range(6)
    ]

    out_rows = w_out.shape[0] // n_s
    out_mine = lax.dynamic_index_in_dim(
        w_out.reshape(n_s, out_rows, width), s_at, 0, keepdims=False
    )
    out_quarter = lax.all_gather(out_mine, "fsdp", axis=0)
    up_mine = lax.dynamic_index_in_dim(
        w_up.reshape(shard, n_f, n_s, ff_q), s_at, 2, keepdims=False
    ).reshape(shard, n_f * ff_q)
    full_up = lax.all_gather(up_mine, "fsdp", axis=0, tiled=True)
    down_mine = lax.dynamic_index_in_dim(
        w_down.reshape(n_s, ff_q, width), s_at, 0, keepdims=False
    )
    full_down = lax.all_gather(down_mine, "fsdp", axis=0, tiled=True)
    out_heads = lax.all_to_all(
        out_quarter.reshape(n_s, n_f // n_s, out_rows, width), "seq", 0, 0, tiled=True
    )
    full_out = out_heads.transpose(1, 0, 2, 3).reshape(inner, width)

    source = tokens.reshape(seq_loc, width).astype(F32)
    grad_y = grad_output.reshape(seq_loc, width).astype(F32)
    normed1, inv1 = layer_norm(source)
    hidden1 = (normed1 * (1.0 + scale_attn) + shift_attn).astype(BF)
    hidden1_all = gather_seq(hidden1, n_s)
    grad_ff = grad_y * gate_ff
    grad_ff_all = gather_seq(grad_ff.astype(BF), n_s)
    part, qkv, mix, lse = attn_forward(hidden1_all, full_qkv, bias_qkv, full_out)
    attn_out = scatter_seq(part, n_s) + full_bout
    resid1 = source + gate_attn * attn_out
    normed2, inv2 = layer_norm(resid1)
    hidden2 = (normed2 * (1.0 + scale_ff) + shift_ff).astype(BF)
    hidden2_all = gather_seq(hidden2, n_s)
    ff_part, gh2_part, gw_up, gw_down, gb_up = feed_forward(
        hidden2_all, grad_ff_all, full_up, bias_up, full_down
    )
    grad_h2 = scatter_seq(gh2_part, n_s)
    s_down = lax.psum_scatter(gw_down, "fsdp", scatter_dimension=0, tiled=True)
    s_up = lax.psum_scatter(gw_up, "fsdp", scatter_dimension=0, tiled=True)

    grad_resid1 = grad_y + norm_back(grad_h2 * (1.0 + scale_ff), normed2, inv2)
    grad_attn = grad_resid1 * gate_attn
    grad_attn_all = gather_seq(grad_attn.astype(BF), n_s)
    ff_out = scatter_seq(ff_part, n_s) + full_bdown
    output = (resid1 + gate_ff * ff_out).astype(BF)
    gh1_part, gw_qkv, gw_out, gb_qkv = attn_backward(
        grad_attn_all, hidden1_all, full_qkv, full_out, qkv, mix, lse
    )
    grad_h1 = scatter_seq(gh1_part, n_s)
    s_qkv = lax.psum_scatter(gw_qkv, "fsdp", scatter_dimension=0, tiled=True)
    gw_out_q = lax.all_to_all(
        gw_out.reshape(n_f // n_s, n_s, out_rows, width).transpose(1, 0, 2, 3),
        "seq", 0, 0, tiled=True,
    )
    s_out = lax.psum_scatter(
        gw_out_q.reshape(n_f * out_rows, width), "fsdp", scatter_dimension=0, tiled=True
    )
    grad_tokens = (grad_resid1 + norm_back(grad_h1 * (1.0 + scale_attn), normed1, inv1)).astype(BF)

    token_sums = [
        grad_h1, grad_h1 * normed1, grad_resid1 * attn_out, grad_h2, grad_h2 * normed2,
        grad_y * ff_out,
    ]
    grad_mods = jnp.concatenate([jnp.sum(value, axis=0) for value in token_sums])
    grad_mods = grad_mods.astype(BF).astype(F32)
    gb_qv = jnp.stack([gb_qkv[0, :inner], gb_qkv[0, 2 * inner :]]).reshape(2, 1, inner)
    gb_qv = lax.dynamic_update_slice(jnp.zeros((2, n_s, inner), F32), gb_qv, (0, s_at, 0))
    gb_up_full = lax.dynamic_update_slice(
        jnp.zeros((n_f, n_s, ff_q), F32), gb_up.reshape(n_f, 1, ff_q), (0, s_at, 0)
    )
    small = jnp.concatenate(
        [grad_mods, jnp.sum(grad_ff, axis=0), jnp.sum(grad_attn, axis=0), gb_up_full.reshape(-1),
         gb_qv.reshape(-1)]
    )
    small_all = lax.all_gather(lax.psum(small, "seq"), "fsdp", axis=0)
    mods_all = small_all[:, :mods_width]
    total = jnp.sum(small_all, axis=0)
    parts, start = [], 0
    for size in (mods_width, width, width, ff_width):
        piece = size // n_f
        parts.append(lax.dynamic_slice(total, (start + f_at * piece,), (piece,)))
        start += size
    t_bada, t_bdown, t_bout, t_bup = parts
    t_bqv = lax.dynamic_slice(
        total[start:].reshape(2, attn_width), (0, f_at * (attn_width // n_f)), (2, attn_width // n_f)
    )
    mods_low = mods_all.astype(BF)
    t_wada = dot_tn(act_rows, mods_low)
    cond_rows = dot_nt(mods_low, w_ada)
    grad_act = lax.all_gather(cond_rows, "fsdp", axis=1, tiled=True)
    grad_act = lax.dynamic_slice_in_dim(grad_act, f_at, 1, 0)
    cond_sig = jax.nn.sigmoid(condition)
    t_cond = grad_act * cond_sig * (1.0 + condition * (1.0 - cond_sig))

    a_down = lax.all_gather(s_down, "seq", axis=0, tiled=True)
    a_up = lax.all_gather(s_up, "seq", axis=0)
    a_qkv = lax.all_gather(s_qkv, "seq", axis=0)
    a_out = lax.all_gather(s_out, "seq", axis=0, tiled=True)
    t_wup = a_up.reshape(n_s, shard, n_f, ff_q).transpose(1, 2, 0, 3).reshape(shard, ff_width)
    t_wqkv = a_qkv.reshape(n_s, shard, 3, inner).transpose(1, 2, 0, 3).reshape(shard, -1)
    return (
        output[None],
        grad_tokens[None],
        t_cond,
        t_wada,
        t_bada,
        t_wqkv.astype(F32),
        t_bqv,
        a_out.astype(F32),
        t_bout,
        t_wup.astype(F32),
        t_bup,
        a_down.astype(F32),
        t_bdown,
    )


def solution(mesh):
    in_specs = (
        P("fsdp", "seq", None),
        P("fsdp", None),
        P("fsdp", None),
        P("fsdp"),
        P("fsdp", None),
        P(None, "fsdp"),
        P("fsdp", None),
        P("fsdp"),
        P("fsdp", None),
        P("fsdp"),
        P("fsdp", None),
        P("fsdp"),
        P("fsdp", "seq", None),
    )
    out_specs = (
        P("fsdp", "seq", None),
        P("fsdp", "seq", None),
        P("fsdp", None),
        P("fsdp", None),
        P("fsdp"),
        P("fsdp", None),
        P(None, "fsdp"),
        P("fsdp", None),
        P("fsdp"),
        P("fsdp", None),
        P("fsdp"),
        P("fsdp", None),
        P("fsdp"),
    )
    body = functools.partial(local, mesh.shape["fsdp"], mesh.shape["seq"])
    return jax.shard_map(body, mesh=mesh, in_specs=in_specs, out_specs=out_specs, check_vma=False)
```

time: 1840 us -> 714 us (0.39)
  blocking collectives: 741 us -> 188 us
  waiting for transfers between devices: 506 us -> 261 us
  matrix products: 152 us -> 4.3 us
  starting transfers between devices: 123 us -> 20.5 us
  local copies, waits for them, and re-layouts: 183 us -> 89.7 us
  Pallas kernels: 0 us -> 81.3 us
  other arithmetic: 95.9 us -> 44 us
    unnamed x3 -> x1, blocking collectives: 653 us -> 29.8 us
    all_gather x7 -> x5, waiting for transfers between devices: 479 us -> 16.4 us  [the longest x1 16.4 us: local(): full_down = lax.all_gather(down_mine, 'fsdp', axis=0, tiled=True)]
    dot_general x20 -> x3, matrix products: 152 us -> 4.3 us  [the longest x1 2.65 us: dot_tn(): lax.dot_general(left, right, (((0,), (0,)), ((), ())), preferred_element_...]
    unnamed x177 -> x111, local copies, waits for them, and re-layouts: 114 us -> 8.46 us
    reduce_scatter x2 -> x3, waiting for transfers between devices: 0.02 us -> 101 us  [the longest x1 73 us: local(): s_down = lax.psum_scatter(gw_down, 'fsdp', scatter_dimension=0, tiled=True)]
    unnamed x20 -> x3, starting transfers between devices: 93.5 us -> 4.2 us
    pallas_call x0 -> x3, Pallas kernels: none -> 81.3 us  [the longest x1 31.1 us: attn_backward(): pl.pallas_call(functools.partial(attn_back_kernel, heads, 256), out_shape...]
    all_gather x4 -> x6, blocking collectives: 66.6 us -> 146 us  [the longest x1 34.3 us: local(): out_quarter = lax.all_gather(out_mine, 'fsdp', axis=0)]
  transfers between devices with their start and end apart: 37 -> 29, of which waited for: 8 -> 15; matrix products, arithmetic and copies ran while one was open for 54% -> 20% of each run, Pallas kernels for 0% -> 7%
where the time goes in v1:
time: 714 us; the launch traced here: 705 us
  waiting for transfers between devices  261 us (37%)
  blocking collectives  188 us (26%)
  local copies, waits for them, and re-layouts  89.7 us (13%)
  Pallas kernels  81.3 us (11%)
  other arithmetic  44 us (6%)
  starting transfers between devices  20.5 us (3%)
  between operations  15.8 us (2%)
    reduce_scatter x1, waiting for transfers between devices, local(): s_down = lax.psum_scatter(gw_down, 'fsdp', scatter_dimension=0, tiled=True)  73 us
    ppermute x16, waiting for transfers between devices, swap(): return lax.ppermute(values, 'seq', [(i, i ^ bit) for i in range(count)])  70.6 us
    unnamed x12, waiting for transfers between devices  53.7 us
    all_gather x1, blocking collectives, local(): out_quarter = lax.all_gather(out_mine, 'fsdp', axis=0)  34.3 us
    all_gather x1, blocking collectives, local(): packed_all = lax.all_gather(packed, 'fsdp', axis=0)  32.4 us
    all_gather x1, blocking collectives, local(): small_all = lax.all_gather(lax.psum(small, 'seq'), 'fsdp', axis=0)  32.2 us
    pallas_call x1, Pallas kernels, attn_backward(): pl.pallas_call(functools.partial(attn_back_kernel, heads, 256), out_shape...  31.1 us
    all_gather x1, blocking collectives, local(): grad_act = lax.all_gather(cond_rows, 'fsdp', axis=1, tiled=True)  30.6 us
  transfers between devices with their start and end apart: 29, of which 15 were waited for; matrix products, arithmetic and copies ran while one was open for 20% of the time, Pallas kernels for 7%

profile of v1, /device:TPU:0, one launch (start us, length us, event | category | flops | bytes accessed | tf_op | source)
XLA Modules:
  0.0 704.7 jit_solution(17336969861481469263)
XLA Ops:
  8.8 2.1 concatenate.41
  11.0 32.4 %all-gather.4 = f32[8,1,2304]{2,1,0:T(1,128)S(1)} all-gather(f32[1,1,2304]{2,1,0:T(1,128)S(1)} %reshape.209), channel_id=2, replica_groups=mesh['fsdp'=8,'seq'=4] {'fsdp'}, dimensions={0}, use_global_device_ids=true | all-gather | bytes 82944 | tf_op jit(solution)/shard_map/all_gather | solution.py:311
  46.1 1.9 reshape.176
  48.1 3.0 dynamic-slice_reduce_fusion.1
  51.1 2.0 reshape.177
  53.2 5.9 reshape.183
  59.0 5.5 dynamic-slice_reduce_fusion
  66.9 51.1 %all-reduce.5.cloned.1.call-done = f32[8,6912]{1,0:T(8,128)} async-done(((f32[8,6912]{1,0:T(8,128)}), f32[8,6912]{1,0:T(8,128)}) %all-reduce.5.cloned.1.call-update) | async-done | bytes 221200
  118.0 2.3 dynamic-slice_reduce_fusion.4
  120.6 1.5 collective-permute-start
  122.1 11.7 %collective-permute-done = bf16[256,1152]{1,0:T(8,128)(2,1)S(1)} collective-permute-done((bf16[256,1152]{1,0:T(8,128)(2,1)S(1)}, bf16[256,1152]{1,0:T(8,128)(2,1)S(1)}, u32[]{:S(2)}, u32[]{:S(2)}) %collective-permute-start) | collective-permute-done | bytes 589856 | tf_op jit(solution)/shard_map/ppermute | solution.py:270
  136.0 34.3 %all_gather.49 = bf16[8,36,1152]{2,1,0:T(8,128)(2,1)S(1)} all-gather(bf16[1,36,1152]{2,1,0:T(8,128)(2,1)S(1)} %constant_dynamic-slice_fusion.3), channel_id=1, replica_groups=mesh['fsdp'=8,'seq'=4] {'fsdp'}, dimensions={0}, use_global_device_ids=true | all-gather | bytes 746496 | tf_op jit(solution)/shard_map/all_gather | solution.py:344
  171.7 4.2 all-to-all-start
  176.8 9.4 %all-to-all-done = bf16[4,2,36,1152]{3,1,2,0:T(2,128)(2,1)} async-done(((bf16[4,2,36,1152]{3,1,2,0:T(2,128)(2,1)}), bf16[4,2,36,1152]{3,1,2,0:T(2,128)(2,1)}, u32[]{:S(2)}, u32[]{:S(2)}) %all-to-all-start) | async-done | bytes 663584 | tf_op jit(solution)/shard_map/all_to_all | solution.py:353
  186.2 2.1 copy.55
  188.3 2.0 reshape.182.wo_ref
  190.3 2.9 pad_maximum_fusion.h_ref
  193.2 21.1 %attn_forward.1 = (bf16[1024,1152]{1,0:T(8,128)(2,1)}, bf16[12,1024,72]{2,1,0:T(8,128)(2,1)}, bf16[1024,288]{1,0:T(8,128)(2,1)}, f32[1024,4]{1,0:T(8,128)}) custom-call(bf16[1024,1152]{1,0:T(8,128)(2,1)} %pad_maximum_fusion.h_ref, bf16[1152,864]{1,0:T(8,128)(2,1)} %all-gather.14.cloned.1.call-done.w_ref, f32[1,864]{1,0:T(1,128)} %broadcast_in_dim.13.b_ref, ...), custom_call_target="tpu_custom_call" | custom-call | flops 4865392640 | bytes 10321920 | tf_op jit(solution)/shard_map/attn_forward/pallas_call | solution.py:86
  214.3 2.4 slice.120
  216.7 1.7 constant_dynamic-slice_fusion.2
  219.7 1.6 add_convert_fusion.3
  223.9 1.7 collective-permute-start.6
  225.6 14.0 %collective-permute-done.3 = bf16[256,1152]{1,0:T(8,128)(2,1)S(1)} collective-permute-done((bf16[256,1152]{1,0:T(8,128)(2,1)}, bf16[256,1152]{1,0:T(8,128)(2,1)S(1)}, u32[]{:S(2)}, u32[]{:S(2)}) %collective-permute-start.3) | collective-permute-done | bytes 589856 | tf_op jit(solution)/shard_map/ppermute | solution.py:270
  240.4 1.7 fusion.42
  243.5 8.7 %collective-permute-done.6 = bf16[256,1152]{1,0:T(8,128)(2,1)S(1)} collective-permute-done((bf16[256,1152]{1,0:T(8,128)(2,1)S(1)}, bf16[256,1152]{1,0:T(8,128)(2,1)S(1)}, u32[]{:S(2)}, u32[]{:S(2)}) %collective-permute-start.6) | collective-permute-done | bytes 589856 | tf_op jit(solution)/shard_map/ppermute | solution.py:270
  253.5 10.5 %collective-permute-done.4 = bf16[256,1152]{1,0:T(8,128)(2,1)S(1)} collective-permute-done((bf16[256,1152]{1,0:T(8,128)(2,1)S(1)}, bf16[256,1152]{1,0:T(8,128)(2,1)S(1)}, u32[]{:S(2)}, u32[]{:S(2)}) %collective-permute-start.4) | collective-permute-done | bytes 589856 | tf_op jit(solution)/shard_map/ppermute | solution.py:270
  266.2 3.4 pad_maximum_fusion.2.gf_ref
  269.5 2.8 pad_maximum_fusion.1.h_ref
  272.4 16.4 %all-gather.20.cloned.1.call-done = bf16[1,1152,1152]{2,1,0:T(8,128)(2,1)} async-done(((bf16[1,144,1152]{2,1,0:T(8,128)(2,1)}), bf16[1,1152,1152]{2,1,0:T(8,128)(2,1)}) %all-gather.20.cloned.1.call-update) | async-done | bytes 2654224 | tf_op jit(solution)/shard_map/all_gather | solution.py:352
  288.8 29.1 %feed_forward.1 = (bf16[1024,1152]{1,0:T(8,128)(2,1)}, bf16[1024,1152]{1,0:T(8,128)(2,1)}, bf16[1152,1152]{1,0:T(8,128)(2,1)}, bf16[1152,1152]{1,0:T(8,128)(2,1)}, f32[1,1152]{1,0:T(1,128)}) custom-call(bf16[1024,1152]{1,0:T(8,128)(2,1)} %pad_maximum_fusion.1.h_ref, bf16[1024,1152]{1,0:T(8,128)(2,1)} %pad_maximum_fusion.2.gf_ref, ...), custom_call_target="tpu_custom_call" | custom-call | flops 16307453952 | bytes 20054016 | tf_op jit(solution)/shard_map/feed_forward/pallas_call | solution.py:239
  318.6 1.5 slice.134
  320.8 2.2 collective-permute-done.10
  327.9 12.9 %collective-permute-done.11 = bf16[256,1152]{1,0:T(8,128)(2,1)} collective-permute-done((bf16[256,1152]{1,0:T(8,128)(2,1)}, bf16[256,1152]{1,0:T(8,128)(2,1)}, u32[]{:S(2)}, u32[]{:S(2)}) %collective-permute-start.11) | collective-permute-done | bytes 589856 | tf_op jit(solution)/shard_map/ppermute | solution.py:270
  340.8 2.5 multiply_reduce_fusion
  343.3 9.3 %collective-permute-done.9 = bf16[256,1152]{1,0:T(8,128)(2,1)} collective-permute-done((bf16[256,1152]{1,0:T(8,128)(2,1)}, bf16[256,1152]{1,0:T(8,128)(2,1)}, u32[]{:S(2)}, u32[]{:S(2)}) %collective-permute-start.9) | collective-permute-done | bytes 589856 | tf_op jit(solution)/shard_map/ppermute | solution.py:270
  352.6 4.7 fusion.9
  358.4 1.6 collective-permute-start.12
  360.0 28.4 %reduce-scatter.8.cloned.1.call-done = bf16[144,1152]{1,0:T(8,128)(2,1)} async-done(((bf16[1152,1152]{1,0:T(8,128)(2,1)}), bf16[144,1152]{1,0:T(8,128)(2,1)}) %reduce-scatter.8.cloned.1.call-update) | async-done | bytes 331792 | tf_op jit(solution)/shard_map/reduce_scatter | solution.py:376
  389.7 73.0 %reduce-scatter.10.cloned.1.call-done = bf16[144,1152]{1,0:T(8,128)(2,1)} async-done(((bf16[1152,1152]{1,0:T(8,128)(2,1)}), bf16[144,1152]{1,0:T(8,128)(2,1)}) %reduce-scatter.10.cloned.1.call-update) | async-done | bytes 331792 | tf_op jit(solution)/shard_map/reduce_scatter | solution.py:375
  462.8 2.9 pad_maximum_fusion.3.ga_ref
  465.6 31.1 %attn_backward.1 = (bf16[1024,1152]{1,0:T(8,128)(2,1)}, bf16[1152,864]{1,0:T(8,128)(2,1)}, bf16[288,1152]{1,0:T(8,128)(2,1)}, f32[1,864]{1,0:T(1,128)}) custom-call(bf16[1024,1152]{1,0:T(8,128)(2,1)} %pad_maximum_fusion.3.ga_ref, bf16[1024,1152]{1,0:T(8,128)(2,1)} %pad_maximum_fusion.h_ref, bf16[1152,864]{1,0:T(8,128)(2,1)} %all-gather.14.cloned.1.call-done.w_ref, ...), custom_call_target="tpu_custom_call" | custom-call | flops 10804527104 | bytes 15335424 | tf_op jit(solution)/shard_map/attn_backward/pallas_call | solution.py:168
  496.7 2.4 slice.138
  500.7 3.5 all-to-all-start.1
  505.3 9.1 %all-to-all-done.1 = bf16[4,2,36,1152]{3,1,2,0:T(2,128)(2,1)S(1)} async-done(((bf16[4,2,36,1152]{3,1,2,0:T(2,128)(2,1)}), bf16[4,2,36,1152]{3,1,2,0:T(2,128)(2,1)S(1)}, u32[]{:S(2)}, u32[]{:S(2)}) %all-to-all-start.1) | async-done | bytes 663584 | tf_op jit(solution)/shard_map/all_to_all | solution.py:388
  514.7 1.9 add_convert_fusion
  518.8 29.8 %fusion = bf16[48,1152]{1,0:T(8,128)(2,1)S(1)} fusion(bf16[288,1152]{1,0:T(8,128)(2,1)S(1)} %reshape.193), kind=kCustom, calls=%all-reduce-scatter | all-reduce-scatter fusion | flops 442369 | bytes 774656
  548.7 2.1 collective-permute-start.16
  550.8 2.0 collective-permute-start.17
  553.0 1.9 collective-permute-done.17
  555.6 7.4 %all-gather.7 = bf16[4,36,1152]{2,1,0:T(8,128)(2,1)S(1)} all-gather(bf16[1,36,1152]{2,1,0:T(8,128)(2,1)S(1)} %dynamic-slice_bitcast_fusion), channel_id=1, replica_groups=mesh['fsdp'=8,'seq'=4] {'seq'}, dimensions={0}, use_global_device_ids=true | all-gather | bytes 414720 | tf_op jit(solution)/shard_map/all_gather | solution.py:435
  563.9 2.5 fusion.18
  568.1 12.2 %psum.7 = f32[1,16128]{1,0:T(1,128)S(1)} all-reduce(f32[1,16128]{1,0:T(1,128)S(1)} %all_gather.52), channel_id=1, replica_groups=mesh['fsdp'=8,'seq'=4] {'seq'}, use_global_device_ids=true, to_apply=%region_17.18 | all-reduce | flops 16128 | bytes 129024 | tf_op jit(solution)/shard_map/psum | solution.py:412
  580.3 32.2 %all-gather.5 = f32[8,1,16128]{2,1,0:T(1,128)S(1)} all-gather(f32[1,1,16128]{2,1,0:T(1,128)S(1)} %bitcast.101), channel_id=1, replica_groups=mesh['fsdp'=8,'seq'=4] {'fsdp'}, dimensions={0}, use_global_device_ids=true | all-gather | bytes 580608 | tf_op jit(solution)/shard_map/all_gather | solution.py:412
  613.5 30.6 %all-gather.6 = f32[8,144,8]{1,2,0:T(8,128)S(1)} all-gather(f32[1,144,8]{1,2,0:T(8,128)S(1)} %convolution_bitcast_fusion), channel_id=1, replica_groups=mesh['fsdp'=8,'seq'=4] {'fsdp'}, dimensions={0}, use_global_device_ids=true | all-gather | bytes 41472 | tf_op jit(solution)/shard_map/all_gather | solution.py:427
  647.0 2.7 fusion.30
  650.3 2.4 fusion.28
  652.7 5.4 reshape.200
  658.1 7.5 %copy.64 = f32[144,8,4,144]{3,2,1,0:T(4,128)} copy(f32[144,8,4,144]{3,1,0,2:T(8,128)} %bitcast.91) | data formatting | bytes 5308416 | tf_op jit(solution)/shard_map/convert_element_type | solution.py:448
  665.7 7.2 %reshape.198 = f32[144,4608]{1,0:T(8,128)} reshape(f32[144,8,4,144]{3,2,1,0:T(4,128)} %copy.64) | data formatting | bytes 5308416 | tf_op jit(solution)/shard_map/convert_element_type | solution.py:448
  672.9 3.0 convert_element_type.186
  675.9 9.6 %all-gather.2 = bf16[576,864]{1,0:T(8,128)(2,1)S(1)} all-gather(bf16[144,864]{1,0:T(8,128)(2,1)} %reduce-scatter.6.cloned.1.call-done), channel_id=4, replica_groups=mesh['fsdp'=8,'seq'=4] {'seq'}, dimensions={0}, use_global_device_ids=true | all-gather | bytes 1244160 | tf_op jit(solution)/shard_map/all_gather | solution.py:434
  685.6 3.3 reshape.199
  688.9 5.2 copy.61
  694.1 3.6 reshape.197
  (242 shorter events, 41.5 us)
Async XLA Ops:
  7.2 37.8 %copy-start = (bf16[144,6912]{1,0:T(8,128)(2,1)S(1)}, bf16[144,6912]{1,0:T(8,128)(2,1)}, u32[]{:S(2)}) copy-start(bf16[144,6912]{1,0:T(8,128)(2,1)} %param.15) | copy-start | bytes 5971972
  7.2 110.8 %all-reduce.5.cloned.1.call-start = ((), (), s32[]{:S(2)}) async-start(), calls=%async_computation.13 | async-start | bytes 442368
  46.0 147.1 %all-gather.14.cloned.1.call-start = ((), (), s32[]{:S(2)}) async-start(), calls=%async_computation.5 | async-start | bytes 2322432 | tf_op jit(solution)/shard_map/all_gather | solution.py:305
  53.1 219.3 %all-gather.16.cloned.1.call-start = ((), (), s32[]{:S(2)}) async-start(), calls=%async_computation.6 | async-start | bytes 2985984 | tf_op jit(solution)/shard_map/all_gather | solution.py:348
  59.0 6.8 copy-start.1
  64.5 1.8 copy-start.47
  66.0 69.0 %copy-start.33 = (f32[256]{0:T(256)}, f32[256]{0:T(256)S(1)}, u32[]{:S(2)}) copy-start(f32[256]{0:T(256)S(1)} %broadcast_multiply_fusion.5) | copy-start | bytes 3076
  66.9 68.0 %copy-start.40 = (f32[256]{0:T(256)}, f32[256]{0:T(256)S(1)}, u32[]{:S(2)}) copy-start(f32[256]{0:T(256)S(1)} %add_rsqrt_fusion.1) | copy-start | bytes 3076
  120.6 13.3 %collective-permute-start = (bf16[256,1152]{1,0:T(8,128)(2,1)S(1)}, bf16[256,1152]{1,0:T(8,128)(2,1)S(1)}, u32[]{:S(2)}, u32[]{:S(2)}) collective-permute-start(bf16[256,1152]{1,0:T(8,128)(2,1)S(1)} %fusion.12), channel_id=1, source_target_pairs={{0,2},{1,3},{2,0},{3,1},{4,6},{5,7},{6,4},{7,5},{8,10},{9,11},{10,... | collective-permute-start | bytes 1769480 | tf_op jit(solution)/shard_map/ppermute | solution.py:270
  135.0 55.3 %collective-permute-start.1 = (bf16[512,1152]{1,0:T(8,128)(2,1)}, bf16[512,1152]{1,0:T(8,128)(2,1)}, u32[]{:S(2)}, u32[]{:S(2)}) collective-permute-start(bf16[512,1152]{1,0:T(8,128)(2,1)} %pad_maximum_fusion.4), channel_id=1, source_target_pairs={{0,1},{1,0},{2,3},{3,2},{4,5},{5,4},{6,7},{7,6},{8,9},{9,8},{10,11... | collective-permute-start | bytes 3538952 | tf_op jit(solution)/shard_map/ppermute | solution.py:270
  170.3 5.6 copy-start.25
  171.7 14.5 %all-to-all-start = ((bf16[4,2,36,1152]{3,1,2,0:T(2,128)(2,1)}), bf16[4,2,36,1152]{3,1,2,0:T(2,128)(2,1)}, u32[]{:S(2)}, u32[]{:S(2)}) async-start(bf16[4,2,36,1152]{3,1,2,0:T(2,128)(2,1)} %copy.54), calls=%async_computation | async-start | bytes 1327104 | tf_op jit(solution)/shard_map/all_to_all | solution.py:353
  175.9 112.9 %all-gather.20.cloned.1.call-start = ((), (), s32[]{:S(2)}) async-start(), calls=%async_computation.11 | async-start | bytes 2985984 | tf_op jit(solution)/shard_map/all_gather | solution.py:352
  216.7 3.1 collective-permute-start.2
  218.4 170.0 %reduce-scatter.8.cloned.1.call-start = ((), (), s32[]{:S(2)}) async-start(), calls=%async_computation.8 | async-start | bytes 2985984 | tf_op jit(solution)/shard_map/reduce_scatter | solution.py:376
  222.3 1.4 copy-start.27
  223.2 16.4 %collective-permute-start.3 = (bf16[256,1152]{1,0:T(8,128)(2,1)}, bf16[256,1152]{1,0:T(8,128)(2,1)S(1)}, u32[]{:S(2)}, u32[]{:S(2)}) collective-permute-start(bf16[256,1152]{1,0:T(8,128)(2,1)} %slice.149), channel_id=1, source_target_pairs={{0,2},{1,3},{2,0},{3,1},{4,6},{5,7},{6,4},{7,5},{8,10},{9,11},{10,... | collective-permute-start | bytes 1769480 | tf_op jit(solution)/shard_map/ppermute | solution.py:270
  223.7 16.7 %copy-start.6 = (bf16[512,1152]{1,0:T(8,128)(2,1)S(1)}, bf16[512,1152]{1,0:T(8,128)(2,1)}, u32[]{:S(2)}) copy-start(bf16[512,1152]{1,0:T(8,128)(2,1)} %copy-done.5) | copy-start | bytes 3538948
  223.9 28.4 %copy-start.12 = (bf16[256,1152]{1,0:T(8,128)(2,1)}, bf16[256,1152]{1,0:T(8,128)(2,1)S(1)}, u32[]{:S(2)}) copy-start(bf16[256,1152]{1,0:T(8,128)(2,1)S(1)} %fusion.10) | copy-start | bytes 1769476
  223.9 28.4 %collective-permute-start.6 = (bf16[256,1152]{1,0:T(8,128)(2,1)S(1)}, bf16[256,1152]{1,0:T(8,128)(2,1)S(1)}, u32[]{:S(2)}, u32[]{:S(2)}) collective-permute-start(bf16[256,1152]{1,0:T(8,128)(2,1)S(1)} %fusion.10), channel_id=1, source_target_pairs={{0,2},{1,3},{2,0},{3,1},{4,6},{5,7},{6,4},{7,5},{8,10},{9,11},{10,... | collective-permute-start | bytes 1769480 | tf_op jit(solution)/shard_map/ppermute | solution.py:270
  243.1 20.9 %copy-start.13 = (bf16[256,1152]{1,0:T(8,128)(2,1)}, bf16[256,1152]{1,0:T(8,128)(2,1)S(1)}, u32[]{:S(2)}) copy-start(bf16[256,1152]{1,0:T(8,128)(2,1)S(1)} %add_convert_fusion.5) | copy-start | bytes 1769476
  243.1 20.9 %collective-permute-start.4 = (bf16[256,1152]{1,0:T(8,128)(2,1)S(1)}, bf16[256,1152]{1,0:T(8,128)(2,1)S(1)}, u32[]{:S(2)}, u32[]{:S(2)}) collective-permute-start(bf16[256,1152]{1,0:T(8,128)(2,1)S(1)} %add_convert_fusion.5), channel_id=1, source_target_pairs={{0,2},{1,3},{2,0},{3,1},{4,6},{5,7},{6,4},{7,5},{8,10},{9,11},{10,... | collective-permute-start | bytes 1769480 | tf_op jit(solution)/shard_map/ppermute | solution.py:270
  253.5 12.7 %collective-permute-start.7 = (bf16[512,1152]{1,0:T(8,128)(2,1)}, bf16[512,1152]{1,0:T(8,128)(2,1)}, u32[]{:S(2)}, u32[]{:S(2)}) collective-permute-start(bf16[512,1152]{1,0:T(8,128)(2,1)} %pad_maximum_fusion.6), channel_id=1, source_target_pairs={{0,1},{1,0},{2,3},{3,2},{4,5},{5,4},{6,7},{7,6},{8,9},{9,8},{10,11... | collective-permute-start | bytes 3538952 | tf_op jit(solution)/shard_map/ppermute | solution.py:270
  265.3 4.3 collective-permute-start.5
  266.2 3.4 copy-start.14
  266.2 3.4 copy-start.20
  317.9 144.8 %reduce-scatter.10.cloned.1.call-start = ((), (), s32[]{:S(2)}) async-start(), calls=%async_computation.9 | async-start | bytes 2985984 | tf_op jit(solution)/shard_map/reduce_scatter | solution.py:375
  318.5 334.2 %all-gather.22.cloned.1.call-start = ((), (), s32[]{:S(2)}) async-start(), calls=%async_computation.12 | async-start | bytes 1658880 | tf_op jit(solution)/shard_map/all_gather | solution.py:433
  318.6 2.0 copy-start.21
  320.1 2.9 collective-permute-start.10
  320.6 2.4 copy-start.22
  320.7 5.0 collective-permute-start.8
  323.3 2.7 copy-start.10
  324.3 16.5 %collective-permute-start.11 = (bf16[256,1152]{1,0:T(8,128)(2,1)}, bf16[256,1152]{1,0:T(8,128)(2,1)}, u32[]{:S(2)}, u32[]{:S(2)}) collective-permute-start(bf16[256,1152]{1,0:T(8,128)(2,1)} %slice.156), channel_id=1, source_target_pairs={{0,2},{1,3},{2,0},{3,1},{4,6},{5,7},{6,4},{7,5},{8,10},{9,11},{10,... | collective-permute-start | bytes 1769480 | tf_op jit(solution)/shard_map/ppermute | solution.py:270
  327.2 25.3 %collective-permute-start.9 = (bf16[256,1152]{1,0:T(8,128)(2,1)}, bf16[256,1152]{1,0:T(8,128)(2,1)}, u32[]{:S(2)}, u32[]{:S(2)}) collective-permute-start(bf16[256,1152]{1,0:T(8,128)(2,1)} %slice.153), channel_id=1, source_target_pairs={{0,2},{1,3},{2,0},{3,1},{4,6},{5,7},{6,4},{7,5},{8,10},{9,11},{10,... | collective-permute-start | bytes 1769480 | tf_op jit(solution)/shard_map/ppermute | solution.py:270
  327.9 24.7 %copy-start.7 = (bf16[512,1152]{1,0:T(8,128)(2,1)S(1)}, bf16[512,1152]{1,0:T(8,128)(2,1)}, u32[]{:S(2)}) copy-start(bf16[512,1152]{1,0:T(8,128)(2,1)} %copy-done.5) | copy-start | bytes 3538948
  327.9 24.7 %copy-start.11 = (bf16[512,1152]{1,0:T(8,128)(2,1)S(1)}, bf16[512,1152]{1,0:T(8,128)(2,1)}, u32[]{:S(2)}) copy-start(bf16[512,1152]{1,0:T(8,128)(2,1)} %copy-done.10) | copy-start | bytes 3538948
  358.4 30.2 %collective-permute-start.12 = (bf16[256,1152]{1,0:T(8,128)(2,1)S(1)}, bf16[256,1152]{1,0:T(8,128)(2,1)S(1)}, u32[]{:S(2)}, u32[]{:S(2)}) collective-permute-start(bf16[256,1152]{1,0:T(8,128)(2,1)S(1)} %multiply_convert_fusion), channel_id=1, source_target_pairs={{0,2},{1,3},{2,0},{3,1},{4,6},{5,7},{6,4},{7,5},{8,10},{9,11},{10,... | collective-permute-start | bytes 1769480 | tf_op jit(solution)/shard_map/ppermute | solution.py:270
  388.4 284.5 %all-gather.18.cloned.1.call-start = ((), (), s32[]{:S(2)}) async-start(), calls=%async_computation.10 | async-start | bytes 1658880 | tf_op jit(solution)/shard_map/all_gather | solution.py:432
  389.7 73.0 %collective-permute-start.13 = (bf16[512,1152]{1,0:T(8,128)(2,1)}, bf16[512,1152]{1,0:T(8,128)(2,1)}, u32[]{:S(2)}, u32[]{:S(2)}) collective-permute-start(bf16[512,1152]{1,0:T(8,128)(2,1)} %pad_maximum_fusion.7), channel_id=1, source_target_pairs={{0,1},{1,0},{2,3},{3,2},{4,5},{5,4},{6,7},{7,6},{8,9},{9,8},{10,11... | collective-permute-start | bytes 3538952 | tf_op jit(solution)/shard_map/ppermute | solution.py:270
  496.7 2.5 copy-start.23
  499.2 15.5 %collective-permute-start.14 = (bf16[512,1152]{1,0:T(8,128)(2,1)}, bf16[512,1152]{1,0:T(8,128)(2,1)}, u32[]{:S(2)}, u32[]{:S(2)}) collective-permute-start(bf16[512,1152]{1,0:T(8,128)(2,1)} %slice.138), channel_id=1, source_target_pairs={{0,1},{1,0},{2,3},{3,2},{4,5},{5,4},{6,7},{7,6},{8,9},{9,8},{10,11... | collective-permute-start | bytes 3538952 | tf_op jit(solution)/shard_map/ppermute | solution.py:270
  499.3 5.6 copy-start.43
  500.7 13.8 %all-to-all-start.1 = ((bf16[4,2,36,1152]{3,1,2,0:T(2,128)(2,1)}), bf16[4,2,36,1152]{3,1,2,0:T(2,128)(2,1)S(1)}, u32[]{:S(2)}, u32[]{:S(2)}) async-start(bf16[4,2,36,1152]{3,1,2,0:T(2,128)(2,1)} %copy.62), calls=%async_computation.2 | async-start | bytes 1327104 | tf_op jit(solution)/shard_map/all_to_all | solution.py:388
  504.2 171.8 %reduce-scatter.6.cloned.1.call-start = ((), (), s32[]{:S(2)}) async-start(), calls=%async_computation.7 | async-start | bytes 2322432 | tf_op jit(solution)/shard_map/reduce_scatter | solution.py:387
  518.5 45.4 %collective-permute-start.15 = (bf16[256,1152]{1,0:T(8,128)(2,1)}, bf16[256,1152]{1,0:T(8,128)(2,1)}, u32[]{:S(2)}, u32[]{:S(2)}) collective-permute-start(bf16[256,1152]{1,0:T(8,128)(2,1)} %slice.158), channel_id=1, source_target_pairs={{0,2},{1,3},{2,0},{3,1},{4,6},{5,7},{6,4},{7,5},{8,10},{9,11},{10,... | collective-permute-start | bytes 1769480 | tf_op jit(solution)/shard_map/ppermute | solution.py:270
  548.7 6.3 collective-permute-start.16
  550.8 4.2 collective-permute-start.17
  552.8 11.1 %copy-start.2 = (bf16[1,256,1152]{2,1,0:T(8,128)(2,1)S(1)}, bf16[1,256,1152]{2,1,0:T(8,128)(2,1)}, u32[]{:S(2)}) copy-start(bf16[1,256,1152]{2,1,0:T(8,128)(2,1)} %param.13) | copy-start | bytes 1769476
  552.9 11.1 %copy-start.34 = (f32[256]{0:T(256)S(1)}, f32[256]{0:T(256)}, u32[]{:S(2)}) copy-start(f32[256]{0:T(256)} %copy-done.33) | copy-start | bytes 3076
  552.9 11.1 %copy-start.41 = (f32[256]{0:T(256)S(1)}, f32[256]{0:T(256)}, u32[]{:S(2)}) copy-start(f32[256]{0:T(256)} %copy-done.40) | copy-start | bytes 3076
  563.0 3.4 copy-start.42
  563.0 3.9 copy-start.39
  563.0 4.2 copy-start.37
  563.9 3.6 copy-start.36
  563.9 3.8 copy-start.38
  563.9 4.1 copy-start.30
  563.9 4.1 copy-start.29
  612.9 34.0 %copy-start.45 = (f32[256]{0:T(256)S(1)}, f32[256]{0:T(256)}, u32[]{:S(2)}) copy-start(f32[256]{0:T(256)} %get-tuple-element.42) | copy-start | bytes 3076
  613.0 34.0 %copy-start.44 = (f32[256]{0:T(256)S(1)}, f32[256]{0:T(256)}, u32[]{:S(2)}) copy-start(f32[256]{0:T(256)} %get-tuple-element.43) | copy-start | bytes 3076
  613.0 34.0 %copy-start.32 = (bf16[8,1,144]{2,1,0:T(2,128)(2,1)S(1)}, bf16[8,1,144]{2,1,0:T(2,128)(2,1)}, u32[]{:S(2)}) copy-start(bf16[8,1,144]{2,1,0:T(2,128)(2,1)} %copy-done.31) | copy-start | bytes 6916
  647.0 2.7 copy-start.35
  647.0 3.3 copy-start.4
  647.0 3.3 copy-start.9
  (13 other events, 12.9 us)
Sparse Core Ops, SparseCore 0:
  46.2 71.7 all-reduce.4
  120.7 55.9 all-gather.13
  179.0 54.1 all-gather.15
  235.1 53.5 all-gather.19
  318.1 70.2 reduce-scatter.7
  392.5 70.2 reduce-scatter.9
  464.3 17.2 all-gather.21
  483.2 18.2 all-gather.17
  508.5 73.7 reduce-scatter.5
